TPU v7x, 256 devices: a 8x8x2 block of a 8x8x16 slice. The times are simulated.
256 devices in a mesh: img: 2 (over z), ga: 16 (over y, core), band: 8 (over x).
Axes of the slice: x: 8, y: 8, z: 2, core: 2. Of those that a mesh axis runs over, the one named last changes fastest.
The devices are a block of a 8x8x16 slice.
Arguments:
- orbitals: bfloat16 [1536, 49152], P(('img', 'band'), 'ga'), parts along dimension 0, as said below
- kernel: float32 [49152], P('ga'), may hold values from 0.3 to 3
- block_vectors: bfloat16 [512, 49152], P(('img', 'band'), 'ga'), parts along dimension 0
Outputs:
- ace_vectors: bfloat16 [1536, 49152], P(('img', 'band'), 'ga'), parts along dimension 0
- exchange_block: bfloat16 [512, 49152], P(('img', 'band'), 'ga'), parts along dimension 0
There are 2 independent parts, one for each index of `img`. A program takes and returns all parts, laid end to end along the dimension named above; an argument that names none is the same for every part. Nothing has to cross between parts.
Inputs may be any that keep to these rules, and one draw needn't show every extreme that they name: `orbitals`: the bands of one image are linearly independent, and the block lies largely in their span.
All inputs are finite; a program needn't handle non-finite values.
Results may differ from a plain program's by a relative error of at most 0.02.
Values may be sent and summed in bfloat16 or wider, within the bound.
No kernel may reach another device: no remote copies, remote signals or barrier semaphores. Data moves between devices by JAX's collectives and lax.ppermute only.
A program may use at most 64 MiB of HBM per device.

v0:
```python
import functools

import jax
import jax.numpy as jnp
from jax import lax
from jax.experimental import pallas as pl
from jax.experimental.pallas import tpu as pltpu
from jax.sharding import Mesh
from jax.sharding import PartitionSpec as P


SUB = 8
BLK = 128
TILE = 512
NEAR = 2


def split(a):
    hi = a.astype(jnp.bfloat16)
    return hi, (a - hi.astype(jnp.float32)).astype(jnp.bfloat16)


def dot3(a, b, dims):
    (ah, al), (bh, bl) = a, b
    dot = functools.partial(
        lax.dot_general, dimension_numbers=(dims, ((), ())), preferred_element_type=jnp.float32
    )
    return dot(ah, bh) + (dot(ah, bl) + dot(al, bh))


def dot1(a, b, dims):
    a, b = a.astype(jnp.bfloat16), b.astype(jnp.bfloat16)
    return lax.dot_general(a, b, (dims, ((), ())), preferred_element_type=jnp.float32)


def dot2(a, b, dims):
    both = dot1(jnp.concatenate(split(a), axis=0), b, dims)
    return both[: a.shape[0]] + both[a.shape[0] :]


def wide(x):
    return jnp.broadcast_to(x, (SUB, BLK))


def lanes(x, k):
    return [wide(x[:, k + j : k + j + 1]) for j in range(SUB)]


def total_of(terms):
    while len(terms) > 1:
        odd = [terms[-1]] if len(terms) % 2 else []
        terms = [a + b for a, b in zip(terms[::2], terms[1::2])] + odd
    return terms[0]


def around(x, before, after):
    parts = [jnp.zeros((before, x.shape[1]), x.dtype), x, jnp.zeros((after, x.shape[1]), x.dtype)]
    return jnp.concatenate([part for part in parts if part.shape[0]], axis=0)


def inverse_of_factor(rows, inv):
    sub = lax.broadcasted_iota(jnp.int32, (SUB, BLK), 0)
    at = [sub == j for j in range(SUB)]
    cols = lanes(rows[0], 0)
    for p in range(len(rows)):
        k = p * SUB
        v, g = rows[p], inv[p]
        last = p + 1 == len(rows)
        if not last:
            ahead, below = lanes(rows[p + 1], k + SUB), lanes(rows[p + 1], k)
        out, unit, recips = g, {}, []
        for j in range(SUB):
            pivot, cj = wide(cols[j][j : j + 1]), cols[j]
            recip = 1.0 / pivot
            recips.append(recip)
            for m in range(j + 1, SUB):
                t = wide(cols[m][j : j + 1]) * recip
                unit[j, m] = t
                cols[m] = jnp.where(at[j], t, cols[m] - cj * t)
            gj = wide(g[j : j + 1])
            out = jnp.where(at[j], gj * lax.rsqrt(pivot), out)
            vj, gj = wide(v[j : j + 1]) * recip, gj * recip
            v = jnp.where(at[j], vj, v - cj * vj)
            g = jnp.where(at[j], gj, g - cj * gj)
        inv[p] = out
        if last:
            break
        lower = list(below)
        for j in range(SUB):
            for m in range(j + 1, SUB):
                lower[m] = lower[m] - lower[j] * unit[j, m]
        scaled = [lower[j] * recips[j] for j in range(SUB)]
        cols = [
            ahead[m] - total_of([lower[j] * wide(scaled[j][m : m + 1]) for j in range(SUB)])
            for m in range(SUB)
        ]
        far = min(p + 1 + NEAR, len(rows))
        if far < len(rows):
            pivots = jnp.concatenate([v, g], axis=1)
            zeros = jnp.zeros_like(pivots)
            pivots = [zeros, pivots] if p % 2 else [pivots, zeros]
            first = p // 2 * 2 * SUB
            pivots = jnp.concatenate(pivots, axis=0).astype(jnp.bfloat16)
            pivots = around(pivots, first, BLK - first - 2 * SUB)
            taken = dot1(jnp.concatenate(rows[far:], axis=0), pivots, ((1,), (0,)))
        vs = [wide(v[j : j + 1]) for j in range(SUB)]
        gs = [wide(g[j : j + 1]) for j in range(SUB)]
        for q in range(p + 1, len(rows)):
            if q < far:
                c = below if q == p + 1 else lanes(rows[q], k)
                rows[q] = rows[q] - total_of([c[j] * vs[j] for j in range(SUB)])
                inv[q] = inv[q] - total_of([c[j] * gs[j] for j in range(SUB)])
            else:
                i = (q - far) * SUB
                rows[q] = rows[q] - taken[i : i + SUB, :BLK]
                inv[q] = inv[q] - taken[i : i + SUB, BLK:]
    return inv


def eliminate(a, d_ref, g_ref, r_ref):
    blocks = a.shape[0] // BLK
    row = lax.broadcasted_iota(jnp.int32, (SUB, BLK), 0)
    col = lax.broadcasted_iota(jnp.int32, (SUB, BLK), 1)
    groups = range(BLK // SUB)
    rows_of = ((0,), (0,))

    def block(i):
        return pl.ds(pl.multiple_of(i * BLK, BLK), BLK)

    d_ref[...] = a[:BLK, :BLK]
    r_ref[...] = jnp.zeros(r_ref.shape, jnp.float32)

    def step(b, _):
        rows = [d_ref[SUB * i : SUB * (i + 1), :] for i in groups]
        inv = [jnp.where(col == row + SUB * i, 1.0, 0.0) for i in groups]
        for i, g in enumerate(inverse_of_factor(rows, inv)):
            g_ref[SUB * i : SUB * (i + 1), :] = g
        r = r_ref[...].astype(jnp.bfloat16)
        before = block(lax.rem(b + blocks - 1, blocks))
        for i in range(blocks - 1):
            them = block(lax.rem(b + i, blocks))
            live = jnp.logical_and(b > 0, b + i < blocks)
            factor = jnp.where(live, r_ref[:, them], 0.0)
            a[them, before] = jnp.where(live, 0.0, a[them, before])
            a[them, :] = a[them, :] - dot1(factor, r, rows_of)
        here, after = block(b), block(jnp.minimum(b + 1, blocks - 1))
        g = g_ref[...]
        r_ref[...] = dot3(split(g), split(a[here, :]), ((1,), (0,)))
        factor = r_ref[:, after]
        d_ref[...] = a[after, after] - dot1(factor, factor, rows_of)
        r_ref[:, here] = g
        a[here, :] = r_ref[...]
        return 0

    lax.fori_loop(0, blocks, step, 0)


def project_kernel(count, keys, *refs):
    pieces = refs[6 : 6 + len(keys)]
    band_ref, core_ref, mine_ref, other_ref, s_ref, s_other_ref = refs[:6]
    p_ref, x_ref, w_ref, a_ref, b_ref, d_ref, g_ref, r_ref, sem = refs[6 + len(keys) :]
    n, own = a_ref.shape[0], p_ref.shape[0]
    half = own // 2
    band, core = band_ref[0], core_ref[0]

    copies = []
    for i, ((distance, first, rows), piece) in enumerate(zip(keys, pieces)):
        to = pl.multiple_of(lax.rem(band + distance, count) * own + first, SUB)
        copies.append(pltpu.make_async_copy(piece, w_ref.at[pl.ds(to, rows), :], sem.at[i]))
        copies[-1].start()

    far = count // 2
    used = (far + 1) * own
    lane = lax.broadcasted_iota(jnp.int32, (half, mine_ref.shape[2]), 1)
    twice = (lane < own) | (lane >= far * own)
    weight = jnp.where(lane < used, jnp.where(twice, 0.5, 1.0), 0.0)
    pad = jnp.zeros((half, n - mine_ref.shape[2]), jnp.float32)
    for x in range(count):
        for h in range(2):
            mine, other = mine_ref[x].astype(jnp.float32), other_ref[x].astype(jnp.float32)
            rows = jnp.where(core == h, mine, other)
            rows = jnp.where(lane < used, rows, 0.0) * weight
            rows = jnp.concatenate([rows, pad], axis=1)
            shift = ((x - far) * own) % n
            if shift:
                rows = pltpu.roll(rows, shift, 1)
            at = x * own + h * half
            b_ref[at : at + half, :] = rows
    for i in range(0, n, BLK):
        for j in range(0, n, BLK):
            a_ref[i : i + BLK, j : j + BLK] = (
                b_ref[i : i + BLK, j : j + BLK] + b_ref[j : j + BLK, i : i + BLK].T
            )

    eliminate(a_ref, d_ref, g_ref, r_ref)

    row = lax.broadcasted_iota(jnp.int32, (n, n), 0)
    col = lax.broadcasted_iota(jnp.int32, (n, n), 1)
    inverse = jnp.where(row >= col, a_ref[...], 0.0).astype(jnp.bfloat16)
    overlap = jnp.concatenate(
        [
            jnp.where(core == 0, s_ref[...], s_other_ref[...]),
            jnp.where(core == 0, s_other_ref[...], s_ref[...]),
        ],
        axis=0,
    )
    overlap = pltpu.roll(overlap, lax.rem(band + far, count) * own, 1)
    coupling = dot2(overlap, inverse, ((1,), (1,)))
    applied = -dot2(coupling, inverse, ((1,), (0,)))
    first = pl.multiple_of(band * own, SUB)
    own_row = first + lax.broadcasted_iota(jnp.int32, (own, n), 0)
    own_rows = jnp.where(own_row >= col[:own], a_ref[pl.ds(first, own), :], 0.0)
    coefs = jnp.concatenate([own_rows, applied], axis=0).astype(jnp.bfloat16)

    for copy in copies:
        copy.wait()
    for at in range(0, w_ref.shape[1], TILE):
        out = jnp.dot(coefs, w_ref[:, at : at + TILE], preferred_element_type=jnp.float32)
        out = out.astype(jnp.bfloat16)
        p_ref[:, at : at + TILE] = out[:own]
        x_ref[:, at : at + TILE] = out[own:]


def project(band, core, mine, other, overlap, other_overlap, got, own):
    count = mine.shape[0]
    keys, pieces = list(got), list(got.values())
    n, cols = count * own, pieces[0].shape[1]
    vmem = pl.BlockSpec(memory_space=pltpu.VMEM)
    return pl.pallas_call(
        functools.partial(project_kernel, count, keys),
        out_shape=[
            jax.ShapeDtypeStruct((own, cols), jnp.bfloat16),
            jax.ShapeDtypeStruct((2 * overlap.shape[0], cols), jnp.bfloat16),
        ],
        in_specs=[pl.BlockSpec(memory_space=pltpu.SMEM)] * 2
        + [vmem] * 4
        + [pl.BlockSpec(memory_space=pl.ANY)] * len(pieces),
        out_specs=[vmem, vmem],
        scratch_shapes=[
            pltpu.VMEM((n, cols), jnp.bfloat16),
            pltpu.VMEM((n, n), jnp.float32),
            pltpu.VMEM((n, n), jnp.float32),
            pltpu.VMEM((BLK, BLK), jnp.float32),
            pltpu.VMEM((BLK, BLK), jnp.float32),
            pltpu.VMEM((BLK, n), jnp.float32),
            pltpu.SemaphoreType.DMA((len(pieces),)),
        ],
        name="project",
    )(band[None], core[None], mine, other, overlap, other_overlap, *pieces)


def ring(shard, left):
    count = lax.axis_size("band")
    ways = {s: [(i, (i + s) % count) for i in range(count)] for s in (1, -1)}
    mid = shard.shape[0] // 2
    far = count // 2
    longer = ((1, 0), (-1, 1))

    def dot(piece):
        return lax.dot_general(
            left, piece, (((1,), (1,)), ((), ())), preferred_element_type=jnp.float32
        )

    got = {(0, h * mid, mid): shard[h * mid : (h + 1) * mid] for h in range(2)}
    parts = {key: dot(x) for key, x in got.items()}
    chains = {(way, h): [(0, h * mid, mid)] for way, h in longer + ((1, 1), (-1, 0))}
    for s in range(1, far + 1):
        for (way, h), keys in chains.items():
            if s == far and (way, h) not in longer:
                continue
            x = got[keys[-1]]
            if s > 1 or (way, h) not in longer:
                before = keys[max(s - 2, 0)]
                x, parts[before] = lax.optimization_barrier((x, parts[before]))
            key = ((keys[-1][0] - way) % count, h * mid, mid)
            got[key] = lax.ppermute(x, "band", ways[way])
            keys.append(key)
        if s > 1:
            for (way, h), keys in chains.items():
                parts[keys[s - 1]] = dot(got[keys[s - 1]])
    for way, h in longer:
        keys = chains[way, h]
        parts[keys[far]] = dot(got[keys[far]])
    return got, parts


def to_all(shard, axis):
    count = lax.axis_size(axis)
    return lax.all_to_all(
        jnp.broadcast_to(shard[None], (count, *shard.shape)), axis, 0, 0, tiled=True
    )


def shards(orbitals, kernel, block_vectors):
    band, core, count = lax.axis_index("band"), lax.axis_index("core"), lax.axis_size("band")
    total = orbitals.shape[1] * lax.axis_size("y") * lax.axis_size("core")
    own, mine = orbitals.shape[0], block_vectors.shape[0]
    ho, hb = own // 2, mine // 2
    far = count // 2
    swap = [(0, 1), (1, 0)]

    weighted = (-(orbitals.astype(jnp.float32) * kernel[None, :])).astype(jnp.bfloat16)
    left = jnp.concatenate(
        [orbitals[:ho], block_vectors[:hb], orbitals[ho:], block_vectors[hb:]], axis=0
    )
    got, parts = ring(weighted, left)

    order = sorted(parts, key=lambda key: ((key[0] - far) % count, key[1]))
    partial = jnp.concatenate([parts[key] for key in order], axis=1)
    n = own * count
    rows = ho + hb
    kept = lax.dynamic_slice_in_dim(partial, core * rows, rows, 0)
    sent = lax.dynamic_slice_in_dim(partial, (1 - core) * rows, rows, 0)
    kept = kept + lax.ppermute(sent, "core", swap)

    used = -(-(far + 1) * own // BLK) * BLK
    fold = ho // hb
    cols = n // fold
    packed = jnp.concatenate(
        [
            kept[:ho, :used],
            jnp.concatenate([kept[ho:, i * cols : (i + 1) * cols] for i in range(fold)], axis=0),
        ],
        axis=1,
    )
    summed = to_all(packed.astype(jnp.bfloat16), "y").astype(jnp.float32).sum(axis=0) / total
    margin = to_all((-summed[:, :used]).astype(jnp.bfloat16), "band")
    other_margin = lax.ppermute(margin, "core", swap)
    overlap = jnp.concatenate(
        [summed[i * hb : (i + 1) * hb, used:] for i in range(fold)], axis=1
    )
    other = lax.ppermute(overlap, "core", swap)
    return tuple(project(band, core, margin, other_margin, overlap, other, got, own))


def solution(mesh):
    images, ga, bands = (mesh.shape[a] for a in ("img", "ga", "band"))
    split_mesh = Mesh(
        mesh.devices.reshape(images, ga // 2, 2, bands), ("img", "y", "core", "band")
    )
    rows, cols = ("img", "band"), ("y", "core")

    return jax.shard_map(
        shards,
        mesh=split_mesh,
        in_specs=(P(rows, cols), P(cols), P(rows, cols)),
        out_specs=(P(rows, cols), P(rows, cols)),
        check_vma=False,
    )
```

profile of v0, /device:TPU:513, one launch (start us, length us, event | category | flops | bytes accessed | tf_op | source)
XLA Modules:
  0.0 135.9 jit_solution(6027188139092382194)
XLA Ops:
  0.6 1.2 negate_convert_fusion
  1.9 2.3 %collective-permute-start = (bf16[48,3072]{1,0:T(8,128)(2,1)S(1)}, bf16[48,3072]{1,0:T(8,128)(2,1)S(1)}, u32[]{:S(2)}, u32[]{:S(2)}) collective-permute-start(bf16[48,3072]{1,0:T(8,128)(2,1)S(1)} %get-tuple-element.41.refs_6_), channel_id=1, source_target_pairs={{0,1},{1,2},{2,3},{3,4},{4,5},{5,6},{6,7},{7,0},{8,9},{9,10},{10,1... | collective-permute-start | bytes 884744 | tf_op jit(solution)/shard_map/ppermute | solution.py:276
  4.2 2.3 %collective-permute-start.4 = (bf16[48,3072]{1,0:T(8,128)(2,1)S(1)}, bf16[48,3072]{1,0:T(8,128)(2,1)S(1)}, u32[]{:S(2)}, u32[]{:S(2)}) collective-permute-start(bf16[48,3072]{1,0:T(8,128)(2,1)S(1)} %get-tuple-element.34.refs_7_), channel_id=1, source_target_pairs={{0,7},{1,0},{2,1},{3,2},{4,3},{5,4},{6,5},{7,6},{8,15},{9,8},{10,9... | collective-permute-start | bytes 884744 | tf_op jit(solution)/shard_map/ppermute | solution.py:276
  6.6 0.1 pad_maximum_fusion
  6.7 1.0 fusion.1
  7.7 1.0 fusion.3
  8.7 2.7 %collective-permute-start.11 = (bf16[48,3072]{1,0:T(8,128)(2,1)S(1)}, bf16[48,3072]{1,0:T(8,128)(2,1)S(1)}, u32[]{:S(2)}, u32[]{:S(2)}) collective-permute-start(bf16[48,3072]{1,0:T(8,128)(2,1)S(1)} %get-tuple-element.41.refs_6_), channel_id=1, source_target_pairs={{0,7},{1,0},{2,1},{3,2},{4,3},{5,4},{6,5},{7,6},{8,15},{9,8},{10,9... | collective-permute-start | bytes 884744 | tf_op jit(solution)/shard_map/ppermute | solution.py:276
  11.4 0.1 collective-permute-start.1
  11.4 3.1 %collective-permute-start.5 = (bf16[48,3072]{1,0:T(8,128)(2,1)S(1)}, bf16[48,3072]{1,0:T(8,128)(2,1)S(1)}, u32[]{:S(2)}, u32[]{:S(2)}) collective-permute-start(bf16[48,3072]{1,0:T(8,128)(2,1)S(1)} %collective-permute-done.4.refs_9_), channel_id=1, source_target_pairs={{0,7},{1,0},{2,1},{3,2},{4,3},{5,4},{6,5},{7,6},{8,15},{9,8},{10,9... | collective-permute-start | bytes 884744 | tf_op jit(solution)/shard_map/ppermute | solution.py:276
  14.5 1.1 collective-permute-start.9
  15.7 2.8 %collective-permute-start.12 = (bf16[48,3072]{1,0:T(8,128)(2,1)S(1)}, bf16[48,3072]{1,0:T(8,128)(2,1)S(1)}, u32[]{:S(2)}, u32[]{:S(2)}) collective-permute-start(bf16[48,3072]{1,0:T(8,128)(2,1)S(1)} %collective-permute-done.11.refs_11_), channel_id=1, source_target_pairs={{0,7},{1,0},{2,1},{3,2},{4,3},{5,4},{6,5},{7,6},{8,15},{9,8},{10,9... | collective-permute-start | bytes 884744 | tf_op jit(solution)/shard_map/ppermute | solution.py:276
  18.4 0.4 fusion.10
  18.8 0.4 fusion.12
  19.2 0.0 copy-done.4
  19.2 0.8 collective-permute-start.2
  20.0 0.4 fusion.14
  20.4 0.0 collective-permute-done.5.refs_13_
  20.4 2.9 %collective-permute-start.6 = (bf16[48,3072]{1,0:T(8,128)(2,1)S(1)}, bf16[48,3072]{1,0:T(8,128)(2,1)S(1)}, u32[]{:S(2)}, u32[]{:S(2)}) collective-permute-start(bf16[48,3072]{1,0:T(8,128)(2,1)S(1)} %collective-permute-done.5.refs_13_), channel_id=1, source_target_pairs={{0,7},{1,0},{2,1},{3,2},{4,3},{5,4},{6,5},{7,6},{8,15},{9,8},{10,9... | collective-permute-start | bytes 884744 | tf_op jit(solution)/shard_map/ppermute | solution.py:276
  23.3 0.4 fusion.11
  23.7 0.0 copy-done.8
  23.7 3.8 %collective-permute-done.2.refs_16_ = bf16[48,3072]{1,0:T(8,128)(2,1)S(1)} collective-permute-done((bf16[48,3072]{1,0:T(8,128)(2,1)S(1)}, bf16[48,3072]{1,0:T(8,128)(2,1)S(1)}, u32[]{:S(2)}, u32[]{:S(2)}) %collective-permute-start.2) | collective-permute-done | bytes 294944 | tf_op jit(solution)/shard_map/ppermute | solution.py:276
  27.5 0.2 collective-permute-start.3
  27.7 0.4 fusion.13
  28.1 0.0 copy-done.9
  28.1 2.6 %collective-permute-done.6.refs_17_ = bf16[48,3072]{1,0:T(8,128)(2,1)S(1)} collective-permute-done((bf16[48,3072]{1,0:T(8,128)(2,1)S(1)}, bf16[48,3072]{1,0:T(8,128)(2,1)S(1)}, u32[]{:S(2)}, u32[]{:S(2)}) %collective-permute-start.6) | collective-permute-done | bytes 294944 | tf_op jit(solution)/shard_map/ppermute | solution.py:276
  30.7 2.3 %collective-permute-start.7 = (bf16[48,3072]{1,0:T(8,128)(2,1)S(1)}, bf16[48,3072]{1,0:T(8,128)(2,1)S(1)}, u32[]{:S(2)}, u32[]{:S(2)}) collective-permute-start(bf16[48,3072]{1,0:T(8,128)(2,1)S(1)} %collective-permute-done.6.refs_17_), channel_id=1, source_target_pairs={{0,7},{1,0},{2,1},{3,2},{4,3},{5,4},{6,5},{7,6},{8,15},{9,8},{10,9... | collective-permute-start | bytes 884744 | tf_op jit(solution)/shard_map/ppermute | solution.py:276
  33.0 0.4 fusion.15
  33.4 0.0 collective-permute-done.9.refs_14_
  33.4 3.3 %collective-permute-start.10 = (bf16[48,3072]{1,0:T(8,128)(2,1)S(1)}, bf16[48,3072]{1,0:T(8,128)(2,1)S(1)}, u32[]{:S(2)}, u32[]{:S(2)}) collective-permute-start(bf16[48,3072]{1,0:T(8,128)(2,1)S(1)} %collective-permute-done.9.refs_14_), channel_id=1, source_target_pairs={{0,1},{1,2},{2,3},{3,4},{4,5},{5,6},{6,7},{7,0},{8,9},{9,10},{10,1... | collective-permute-start | bytes 884744 | tf_op jit(solution)/shard_map/ppermute | solution.py:276
  36.7 0.6 collective-permute-start.13
  37.2 0.7 collective-permute-done.3.refs_20_
  37.9 0.4 convolution_dynamic-update-slice_fusion.7
  38.3 3.4 %collective-permute-done.7.refs_21_ = bf16[48,3072]{1,0:T(8,128)(2,1)S(1)} collective-permute-done((bf16[48,3072]{1,0:T(8,128)(2,1)S(1)}, bf16[48,3072]{1,0:T(8,128)(2,1)S(1)}, u32[]{:S(2)}, u32[]{:S(2)}) %collective-permute-start.7) | collective-permute-done | bytes 294944 | tf_op jit(solution)/shard_map/ppermute | solution.py:276
  41.7 0.4 convolution_dynamic-update-slice_fusion.6
  42.1 0.4 convolution_dynamic-update-slice_fusion.5
  42.5 2.2 %collective-permute-done.10.refs_18_ = bf16[48,3072]{1,0:T(8,128)(2,1)S(1)} collective-permute-done((bf16[48,3072]{1,0:T(8,128)(2,1)S(1)}, bf16[48,3072]{1,0:T(8,128)(2,1)S(1)}, u32[]{:S(2)}, u32[]{:S(2)}) %collective-permute-start.10) | collective-permute-done | bytes 294944 | tf_op jit(solution)/shard_map/ppermute | solution.py:276
  44.7 0.4 convolution_dynamic-update-slice_fusion.4
  45.0 0.0 copy-start.22
  45.1 0.4 convolution_dynamic-update-slice_fusion.3
  45.5 0.3 copy-done.22
  45.8 0.0 copy-done.21
  45.8 0.4 convolution_dynamic-update-slice_fusion.2
  46.2 1.8 %collective-permute-done.13.refs_19_ = bf16[48,3072]{1,0:T(8,128)(2,1)S(1)} collective-permute-done((bf16[48,3072]{1,0:T(8,128)(2,1)S(1)}, bf16[48,3072]{1,0:T(8,128)(2,1)S(1)}, u32[]{:S(2)}, u32[]{:S(2)}) %collective-permute-start.13) | collective-permute-done | bytes 294944 | tf_op jit(solution)/shard_map/ppermute | solution.py:276
  48.0 0.4 convolution_dynamic-update-slice_fusion.1
  48.4 0.0 copy-done.13
  48.4 0.4 convolution_dynamic-update-slice_fusion
  48.8 0.2 constant_dynamic-slice_fusion
  48.9 17.5 %collective-permute-start.14 = (f32[64,768]{0,1:T(8,128)S(1)}, f32[64,768]{0,1:T(8,128)S(1)}, u32[]{:S(2)}, u32[]{:S(2)}) collective-permute-start(f32[64,768]{0,1:T(8,128)S(1)} %constant_dynamic-slice_fusion), channel_id=1, source_target_pairs={{0,8},{8,0},{1,9},{9,1},{2,10},{10,2},{3,11},{11,3},{4,12},{12,4},... | collective-permute-start | bytes 589832 | tf_op jit(solution)/shard_map/ppermute | solution.py:314
  66.4 1.3 collective-permute-done.14
  67.8 0.2 add_convert_fusion
  67.9 0.1 fusion.7
  68.1 0.1 copy.10
  68.2 0.1 copy.11
  68.2 0.1 copy.12
  68.3 0.1 copy.13
  68.5 22.7 %all_to_all.10 = bf16[8,48,768]{2,1,0:T(8,128)(2,1)S(1)} all-to-all(bf16[8,48,768]{2,1,0:T(8,128)(2,1)S(1)} %broadcast_in_dim.10), channel_id=1, replica_groups=mesh['img'=2,'y'=8,'core'=2,'band'=8] {'y'}, dimensions={0} | all-to-all | bytes 1179648 | tf_op jit(solution)/shard_map/all_to_all | solution.py:289
  91.3 0.1 convert_reduce_fusion
  91.4 18.3 %all_to_all.11.refs_2_ = bf16[8,48,512]{2,1,0:T(8,128)(2,1)S(1)} all-to-all(bf16[8,48,512]{2,1,0:T(8,128)(2,1)S(1)} %broadcast_in_dim.22), channel_id=1, replica_groups=mesh['img'=2,'y'=8,'core'=2,'band'=8] {'band'}, dimensions={0} | all-to-all | bytes 786432 | tf_op jit(solution)/shard_map/all_to_all | solution.py:289
  109.7 3.0 %collective-permute-start.15 = (bf16[8,48,512]{2,1,0:T(8,128)(2,1)S(1)}, bf16[8,48,512]{2,1,0:T(8,128)(2,1)S(1)}, u32[]{:S(2)}, u32[]{:S(2)}) collective-permute-start(bf16[8,48,512]{2,1,0:T(8,128)(2,1)S(1)} %all_to_all.11.refs_2_), channel_id=1, source_target_pairs={{0,8},{8,0},{1,9},{9,1},{2,10},{10,2},{3,11},{11,3},{4,12},{12,4},... | collective-permute-start | bytes 1179656 | tf_op jit(solution)/shard_map/ppermute | solution.py:328
  112.8 0.1 collective-permute-start.16
  112.9 1.2 collective-permute-done.16.refs_5_
  114.2 0.6 copy-done.23
  114.8 0.2 copy-done.18
  114.9 20.8 %project.1 = (bf16[96,3072]{1,0:T(8,128)(2,1)}, bf16[32,3072]{1,0:T(8,128)(2,1)}) custom-call(s32[1]{0:T(128)} %bitcast.refs_0_, s32[1]{0:T(128)} %bitcast.1.refs_1_, bf16[8,48,512]{2,1,0:T(8,128)(2,1)} %copy-done.1, bf16[8,48,512]{2,1,0:T(8,128)(2,1)} %copy-done.18, f32[16,768]{1,0:T(8,128)} %copy-done.19, f32[16,768]{1,0:T(8,128)} %copy-done.23, ...), custom_call_target="tpu_custom_call" | custom-call | tf_op jit(solution)/shard_map/project/pallas_call | solution.py:229
  (66 shorter events, 0.4 us)
Async XLA Ops:
  1.8 4.7 %copy-start = (bf16[96,3072]{1,0:T(8,128)(2,1)S(1)}, bf16[96,3072]{1,0:T(8,128)(2,1)}, u32[]{:S(2)}) copy-start(bf16[96,3072]{1,0:T(8,128)(2,1)} %param.3) | copy-start | bytes 1769476
  1.9 5.8 %copy-start.2 = (bf16[48,3072]{1,0:T(8,128)(2,1)}, bf16[48,3072]{1,0:T(8,128)(2,1)S(1)}, u32[]{:S(2)}) copy-start(bf16[48,3072]{1,0:T(8,128)(2,1)S(1)} %get-tuple-element.34.refs_7_) | copy-start | bytes 884740
  1.9 6.8 %copy-start.3 = (bf16[48,3072]{1,0:T(8,128)(2,1)}, bf16[48,3072]{1,0:T(8,128)(2,1)S(1)}, u32[]{:S(2)}) copy-start(bf16[48,3072]{1,0:T(8,128)(2,1)S(1)} %get-tuple-element.41.refs_6_) | copy-start | bytes 884740
  1.9 4.7 %copy-start.20 = (bf16[32,3072]{1,0:T(8,128)(2,1)S(1)}, bf16[32,3072]{1,0:T(8,128)(2,1)}, u32[]{:S(2)}) copy-start(bf16[32,3072]{1,0:T(8,128)(2,1)} %param.5) | copy-start | bytes 589828
  1.9 9.4 %collective-permute-start = (bf16[48,3072]{1,0:T(8,128)(2,1)S(1)}, bf16[48,3072]{1,0:T(8,128)(2,1)S(1)}, u32[]{:S(2)}, u32[]{:S(2)}) collective-permute-start(bf16[48,3072]{1,0:T(8,128)(2,1)S(1)} %get-tuple-element.41.refs_6_), channel_id=1, source_target_pairs={{0,1},{1,2},{2,3},{3,4},{4,5},{5,6},{6,7},{7,0},{8,9},{9,10},{10,1... | collective-permute-start | bytes 884744 | tf_op jit(solution)/shard_map/ppermute | solution.py:276
  4.2 7.2 %collective-permute-start.4 = (bf16[48,3072]{1,0:T(8,128)(2,1)S(1)}, bf16[48,3072]{1,0:T(8,128)(2,1)S(1)}, u32[]{:S(2)}, u32[]{:S(2)}) collective-permute-start(bf16[48,3072]{1,0:T(8,128)(2,1)S(1)} %get-tuple-element.34.refs_7_), channel_id=1, source_target_pairs={{0,7},{1,0},{2,1},{3,2},{4,3},{5,4},{6,5},{7,6},{8,15},{9,8},{10,9... | collective-permute-start | bytes 884744 | tf_op jit(solution)/shard_map/ppermute | solution.py:276
  7.7 6.8 %collective-permute-start.8 = (bf16[48,3072]{1,0:T(8,128)(2,1)S(1)}, bf16[48,3072]{1,0:T(8,128)(2,1)S(1)}, u32[]{:S(2)}, u32[]{:S(2)}) collective-permute-start(bf16[48,3072]{1,0:T(8,128)(2,1)S(1)} %get-tuple-element.34.refs_7_), channel_id=1, source_target_pairs={{0,1},{1,2},{2,3},{3,4},{4,5},{5,6},{6,7},{7,0},{8,9},{9,10},{10,1... | collective-permute-start | bytes 884744 | tf_op jit(solution)/shard_map/ppermute | solution.py:276
  8.7 7.0 %collective-permute-start.11 = (bf16[48,3072]{1,0:T(8,128)(2,1)S(1)}, bf16[48,3072]{1,0:T(8,128)(2,1)S(1)}, u32[]{:S(2)}, u32[]{:S(2)}) collective-permute-start(bf16[48,3072]{1,0:T(8,128)(2,1)S(1)} %get-tuple-element.41.refs_6_), channel_id=1, source_target_pairs={{0,7},{1,0},{2,1},{3,2},{4,3},{5,4},{6,5},{7,6},{8,15},{9,8},{10,9... | collective-permute-start | bytes 884744 | tf_op jit(solution)/shard_map/ppermute | solution.py:276
  11.4 7.8 %copy-start.4 = (bf16[48,3072]{1,0:T(8,128)(2,1)}, bf16[48,3072]{1,0:T(8,128)(2,1)S(1)}, u32[]{:S(2)}) copy-start(bf16[48,3072]{1,0:T(8,128)(2,1)S(1)} %collective-permute-done.refs_8_) | copy-start | bytes 884740
  11.4 7.8 %collective-permute-start.1 = (bf16[48,3072]{1,0:T(8,128)(2,1)S(1)}, bf16[48,3072]{1,0:T(8,128)(2,1)S(1)}, u32[]{:S(2)}, u32[]{:S(2)}) collective-permute-start(bf16[48,3072]{1,0:T(8,128)(2,1)S(1)} %collective-permute-done.refs_8_), channel_id=1, source_target_pairs={{0,1},{1,2},{2,3},{3,4},{4,5},{5,6},{6,7},{7,0},{8,9},{9,10},{10,1... | collective-permute-start | bytes 884744 | tf_op jit(solution)/shard_map/ppermute | solution.py:276
  11.4 7.8 %copy-start.5 = (bf16[48,3072]{1,0:T(8,128)(2,1)}, bf16[48,3072]{1,0:T(8,128)(2,1)S(1)}, u32[]{:S(2)}) copy-start(bf16[48,3072]{1,0:T(8,128)(2,1)S(1)} %collective-permute-done.4.refs_9_) | copy-start | bytes 884740
  11.4 8.9 %collective-permute-start.5 = (bf16[48,3072]{1,0:T(8,128)(2,1)S(1)}, bf16[48,3072]{1,0:T(8,128)(2,1)S(1)}, u32[]{:S(2)}, u32[]{:S(2)}) collective-permute-start(bf16[48,3072]{1,0:T(8,128)(2,1)S(1)} %collective-permute-done.4.refs_9_), channel_id=1, source_target_pairs={{0,7},{1,0},{2,1},{3,2},{4,3},{5,4},{6,5},{7,6},{8,15},{9,8},{10,9... | collective-permute-start | bytes 884744 | tf_op jit(solution)/shard_map/ppermute | solution.py:276
  14.5 5.5 %copy-start.6 = (bf16[48,3072]{1,0:T(8,128)(2,1)}, bf16[48,3072]{1,0:T(8,128)(2,1)S(1)}, u32[]{:S(2)}) copy-start(bf16[48,3072]{1,0:T(8,128)(2,1)S(1)} %collective-permute-done.8.refs_10_) | copy-start | bytes 884740
  14.5 18.9 %collective-permute-start.9 = (bf16[48,3072]{1,0:T(8,128)(2,1)S(1)}, bf16[48,3072]{1,0:T(8,128)(2,1)S(1)}, u32[]{:S(2)}, u32[]{:S(2)}) collective-permute-start(bf16[48,3072]{1,0:T(8,128)(2,1)S(1)} %collective-permute-done.8.refs_10_), channel_id=1, source_target_pairs={{0,1},{1,2},{2,3},{3,4},{4,5},{5,6},{6,7},{7,0},{8,9},{9,10},{10,1... | collective-permute-start | bytes 884744 | tf_op jit(solution)/shard_map/ppermute | solution.py:276
  15.7 17.3 %copy-start.7 = (bf16[48,3072]{1,0:T(8,128)(2,1)}, bf16[48,3072]{1,0:T(8,128)(2,1)S(1)}, u32[]{:S(2)}) copy-start(bf16[48,3072]{1,0:T(8,128)(2,1)S(1)} %collective-permute-done.11.refs_11_) | copy-start | bytes 884740
  15.7 21.0 %collective-permute-start.12 = (bf16[48,3072]{1,0:T(8,128)(2,1)S(1)}, bf16[48,3072]{1,0:T(8,128)(2,1)S(1)}, u32[]{:S(2)}, u32[]{:S(2)}) collective-permute-start(bf16[48,3072]{1,0:T(8,128)(2,1)S(1)} %collective-permute-done.11.refs_11_), channel_id=1, source_target_pairs={{0,7},{1,0},{2,1},{3,2},{4,3},{5,4},{6,5},{7,6},{8,15},{9,8},{10,9... | collective-permute-start | bytes 884744 | tf_op jit(solution)/shard_map/ppermute | solution.py:276
  19.2 4.5 %copy-start.8 = (bf16[48,3072]{1,0:T(8,128)(2,1)}, bf16[48,3072]{1,0:T(8,128)(2,1)S(1)}, u32[]{:S(2)}) copy-start(bf16[48,3072]{1,0:T(8,128)(2,1)S(1)} %collective-permute-done.1.refs_12_) | copy-start | bytes 884740
  19.2 8.3 %collective-permute-start.2 = (bf16[48,3072]{1,0:T(8,128)(2,1)S(1)}, bf16[48,3072]{1,0:T(8,128)(2,1)S(1)}, u32[]{:S(2)}, u32[]{:S(2)}) collective-permute-start(bf16[48,3072]{1,0:T(8,128)(2,1)S(1)} %collective-permute-done.1.refs_12_), channel_id=1, source_target_pairs={{0,1},{1,2},{2,3},{3,4},{4,5},{5,6},{6,7},{7,0},{8,9},{9,10},{10,1... | collective-permute-start | bytes 884744 | tf_op jit(solution)/shard_map/ppermute | solution.py:276
  20.4 7.7 %copy-start.9 = (bf16[48,3072]{1,0:T(8,128)(2,1)}, bf16[48,3072]{1,0:T(8,128)(2,1)S(1)}, u32[]{:S(2)}) copy-start(bf16[48,3072]{1,0:T(8,128)(2,1)S(1)} %collective-permute-done.5.refs_13_) | copy-start | bytes 884740
  20.4 10.3 %collective-permute-start.6 = (bf16[48,3072]{1,0:T(8,128)(2,1)S(1)}, bf16[48,3072]{1,0:T(8,128)(2,1)S(1)}, u32[]{:S(2)}, u32[]{:S(2)}) collective-permute-start(bf16[48,3072]{1,0:T(8,128)(2,1)S(1)} %collective-permute-done.5.refs_13_), channel_id=1, source_target_pairs={{0,7},{1,0},{2,1},{3,2},{4,3},{5,4},{6,5},{7,6},{8,15},{9,8},{10,9... | collective-permute-start | bytes 884744 | tf_op jit(solution)/shard_map/ppermute | solution.py:276
  27.5 14.6 %copy-start.12 = (bf16[48,3072]{1,0:T(8,128)(2,1)}, bf16[48,3072]{1,0:T(8,128)(2,1)S(1)}, u32[]{:S(2)}) copy-start(bf16[48,3072]{1,0:T(8,128)(2,1)S(1)} %collective-permute-done.2.refs_16_) | copy-start | bytes 884740
  27.5 10.4 %collective-permute-start.3 = (bf16[48,3072]{1,0:T(8,128)(2,1)S(1)}, bf16[48,3072]{1,0:T(8,128)(2,1)S(1)}, u32[]{:S(2)}, u32[]{:S(2)}) collective-permute-start(bf16[48,3072]{1,0:T(8,128)(2,1)S(1)} %collective-permute-done.2.refs_16_), channel_id=1, source_target_pairs={{0,1},{1,2},{2,3},{3,4},{4,5},{5,6},{6,7},{7,0},{8,9},{9,10},{10,1... | collective-permute-start | bytes 884744 | tf_op jit(solution)/shard_map/ppermute | solution.py:276
  30.7 17.7 %copy-start.13 = (bf16[48,3072]{1,0:T(8,128)(2,1)}, bf16[48,3072]{1,0:T(8,128)(2,1)S(1)}, u32[]{:S(2)}) copy-start(bf16[48,3072]{1,0:T(8,128)(2,1)S(1)} %collective-permute-done.6.refs_17_) | copy-start | bytes 884740
  30.7 11.0 %collective-permute-start.7 = (bf16[48,3072]{1,0:T(8,128)(2,1)S(1)}, bf16[48,3072]{1,0:T(8,128)(2,1)S(1)}, u32[]{:S(2)}, u32[]{:S(2)}) collective-permute-start(bf16[48,3072]{1,0:T(8,128)(2,1)S(1)} %collective-permute-done.6.refs_17_), channel_id=1, source_target_pairs={{0,7},{1,0},{2,1},{3,2},{4,3},{5,4},{6,5},{7,6},{8,15},{9,8},{10,9... | collective-permute-start | bytes 884744 | tf_op jit(solution)/shard_map/ppermute | solution.py:276
  33.4 11.7 %copy-start.10 = (bf16[48,3072]{1,0:T(8,128)(2,1)}, bf16[48,3072]{1,0:T(8,128)(2,1)S(1)}, u32[]{:S(2)}) copy-start(bf16[48,3072]{1,0:T(8,128)(2,1)S(1)} %collective-permute-done.9.refs_14_) | copy-start | bytes 884740
  33.4 11.3 %collective-permute-start.10 = (bf16[48,3072]{1,0:T(8,128)(2,1)S(1)}, bf16[48,3072]{1,0:T(8,128)(2,1)S(1)}, u32[]{:S(2)}, u32[]{:S(2)}) collective-permute-start(bf16[48,3072]{1,0:T(8,128)(2,1)S(1)} %collective-permute-done.9.refs_14_), channel_id=1, source_target_pairs={{0,1},{1,2},{2,3},{3,4},{4,5},{5,6},{6,7},{7,0},{8,9},{9,10},{10,1... | collective-permute-start | bytes 884744 | tf_op jit(solution)/shard_map/ppermute | solution.py:276
  36.7 9.1 %copy-start.11 = (bf16[48,3072]{1,0:T(8,128)(2,1)}, bf16[48,3072]{1,0:T(8,128)(2,1)S(1)}, u32[]{:S(2)}) copy-start(bf16[48,3072]{1,0:T(8,128)(2,1)S(1)} %collective-permute-done.12.refs_15_) | copy-start | bytes 884740
  36.7 11.3 %collective-permute-start.13 = (bf16[48,3072]{1,0:T(8,128)(2,1)S(1)}, bf16[48,3072]{1,0:T(8,128)(2,1)S(1)}, u32[]{:S(2)}, u32[]{:S(2)}) collective-permute-start(bf16[48,3072]{1,0:T(8,128)(2,1)S(1)} %collective-permute-done.12.refs_15_), channel_id=1, source_target_pairs={{0,7},{1,0},{2,1},{3,2},{4,3},{5,4},{6,5},{7,6},{8,15},{9,8},{10,9... | collective-permute-start | bytes 884744 | tf_op jit(solution)/shard_map/ppermute | solution.py:276
  37.9 4.1 %copy-start.14 = (bf16[48,3072]{1,0:T(8,128)(2,1)}, bf16[48,3072]{1,0:T(8,128)(2,1)S(1)}, u32[]{:S(2)}) copy-start(bf16[48,3072]{1,0:T(8,128)(2,1)S(1)} %collective-permute-done.3.refs_20_) | copy-start | bytes 884740
  41.7 0.8 copy-start.15
  44.7 0.8 copy-start.16
  45.0 0.7 copy-start.22
  45.1 0.8 copy-start.21
  48.0 0.8 copy-start.17
  48.9 18.8 %collective-permute-start.14 = (f32[64,768]{0,1:T(8,128)S(1)}, f32[64,768]{0,1:T(8,128)S(1)}, u32[]{:S(2)}, u32[]{:S(2)}) collective-permute-start(f32[64,768]{0,1:T(8,128)S(1)} %constant_dynamic-slice_fusion), channel_id=1, source_target_pairs={{0,8},{8,0},{1,9},{9,1},{2,10},{10,2},{3,11},{11,3},{4,12},{12,4},... | collective-permute-start | bytes 589832 | tf_op jit(solution)/shard_map/ppermute | solution.py:314
  109.7 4.5 %copy-start.1 = (bf16[8,48,512]{2,1,0:T(8,128)(2,1)}, bf16[8,48,512]{2,1,0:T(8,128)(2,1)S(1)}, u32[]{:S(2)}) copy-start(bf16[8,48,512]{2,1,0:T(8,128)(2,1)S(1)} %all_to_all.11.refs_2_) | copy-start | bytes 1179652
  109.7 4.4 %collective-permute-start.15 = (bf16[8,48,512]{2,1,0:T(8,128)(2,1)S(1)}, bf16[8,48,512]{2,1,0:T(8,128)(2,1)S(1)}, u32[]{:S(2)}, u32[]{:S(2)}) collective-permute-start(bf16[8,48,512]{2,1,0:T(8,128)(2,1)S(1)} %all_to_all.11.refs_2_), channel_id=1, source_target_pairs={{0,8},{8,0},{1,9},{9,1},{2,10},{10,2},{3,11},{11,3},{4,12},{12,4},... | collective-permute-start | bytes 1179656 | tf_op jit(solution)/shard_map/ppermute | solution.py:328
  112.8 1.4 %copy-start.19 = (f32[16,768]{1,0:T(8,128)}, f32[16,768]{1,0:T(8,128)S(1)}, u32[]{:S(2)}) copy-start(f32[16,768]{1,0:T(8,128)S(1)} %pad_maximum_fusion.1.refs_4_) | copy-start | bytes 147460
  112.8 1.4 %collective-permute-start.16 = (f32[16,768]{1,0:T(8,128)S(1)}, f32[16,768]{1,0:T(8,128)S(1)}, u32[]{:S(2)}, u32[]{:S(2)}) collective-permute-start(f32[16,768]{1,0:T(8,128)S(1)} %pad_maximum_fusion.1.refs_4_), channel_id=1, source_target_pairs={{0,8},{8,0},{1,9},{9,1},{2,10},{10,2},{3,11},{11,3},{4,12},{12,4},... | collective-permute-start | bytes 147464 | tf_op jit(solution)/shard_map/ppermute | solution.py:332
  114.2 0.6 copy-start.23
  114.2 0.8 copy-start.18
where the time goes:
time: 136 us
  starting transfers between devices  45 us (33%)
  blocking collectives  41.1 us (30%)
  Pallas kernels  20.8 us (15%)
  waiting for transfers between devices  17 us (12%)
  matrix products  7.01 us (5%)
  local copies, waits for them, and re-layouts  2.01 us (1%)
  other arithmetic  1.55 us (1%)
  between operations  1.42 us (1%)
    all_to_all x2, blocking collectives, to_all(): lax.all_to_all(jnp.broadcast_to(shard[None], (count, *shard.shape)), axis...  41.1 us
    ppermute x14, starting transfers between devices, ring(): got[key] = lax.ppermute(x, 'band', ways[way])  24.4 us
    pallas_call x1, Pallas kernels, project(): pl.pallas_call(functools.partial(project_kernel, count, keys), out_shape=...  20.8 us
    ppermute x1, starting transfers between devices, shards(): kept = kept + lax.ppermute(sent, 'core', swap)  17.5 us
    ppermute x14, waiting for transfers between devices, ring(): got[key] = lax.ppermute(x, 'band', ways[way])  14.4 us
    dot_general x16, matrix products, dot(): lax.dot_general(left, piece, (((1,), (1,)), ((), ())), preferred_element_...  7.01 us
    ppermute x1, starting transfers between devices, shards(): other_margin = lax.ppermute(margin, 'core', swap)  3.02 us
  transfers between devices with their start and end apart: 17, of which 8 were waited for; matrix products, arithmetic and copies ran while one was open for 5% of the time, Pallas kernels for 0%

commit v1 on v0

--- a/solution.py
+++ b/solution.py
@@ -269,9 +269,6 @@
             if s == far and (way, h) not in longer:
                 continue
             x = got[keys[-1]]
-            if s > 1 or (way, h) not in longer:
-                before = keys[max(s - 2, 0)]
-                x, parts[before] = lax.optimization_barrier((x, parts[before]))
             key = ((keys[-1][0] - way) % count, h * mid, mid)
             got[key] = lax.ppermute(x, "band", ways[way])
             keys.append(key)
@@ -305,9 +302,11 @@
     )
     got, parts = ring(weighted, left)
 
-    order = sorted(parts, key=lambda key: ((key[0] - far) % count, key[1]))
-    partial = jnp.concatenate([parts[key] for key in order], axis=1)
     n = own * count
+    partial = jnp.zeros((left.shape[0], n), jnp.float32)
+    for (distance, row, _), part in parts.items():
+        at = (distance - far) % count * own + row
+        partial = lax.dynamic_update_slice_in_dim(partial, part, at, 1)
     rows = ho + hb
     kept = lax.dynamic_slice_in_dim(partial, core * rows, rows, 0)
     sent = lax.dynamic_slice_in_dim(partial, (1 - core) * rows, rows, 0)

time: 136 us -> 135 us (level)
  waiting for transfers between devices: 17 us -> 14 us
  starting transfers between devices: 45 us -> 47.5 us
  local copies, waits for them, and re-layouts: 2.01 us -> 4.43 us
  blocking collectives: 41.1 us -> 39.6 us
    ppermute x1, starting transfers between devices: 17.5 us -> 21.7 us  [shards(): kept = kept + lax.ppermute(sent, 'core', swap)]
    ppermute x14, waiting for transfers between devices: 14.4 us -> 11.4 us  [ring(): got[key] = lax.ppermute(x, 'band', ways[way])]
    unnamed x56 -> x44, local copies, waits for them, and re-layouts: 1.21 us -> 3.59 us
    ppermute x14, starting transfers between devices: 24.4 us -> 22.7 us  [ring(): got[key] = lax.ppermute(x, 'band', ways[way])]
    all_to_all x2, blocking collectives: 41.1 us -> 39.6 us  [to_all(): lax.all_to_all(jnp.broadcast_to(shard[None], (count, *shard.shape)), axis...]
  transfers between devices with their start and end apart: 17 -> 17, of which waited for: 8 -> 9; matrix products, arithmetic and copies ran while one was open for 5% -> 4% of each run, Pallas kernels for 0% -> 0%
where the time goes in v1:
time: 135 us
  starting transfers between devices  47.5 us (35%)
  blocking collectives  39.6 us (29%)
  Pallas kernels  20.8 us (15%)
  waiting for transfers between devices  14 us (10%)
  matrix products  5.72 us (4%)
  local copies, waits for them, and re-layouts  4.43 us (3%)
  other arithmetic  1.49 us (1%)
  between operations  1.35 us (1%)
    all_to_all x2, blocking collectives, to_all(): lax.all_to_all(jnp.broadcast_to(shard[None], (count, *shard.shape)), axis...  39.6 us
    ppermute x14, starting transfers between devices, ring(): got[key] = lax.ppermute(x, 'band', ways[way])  22.7 us
    ppermute x1, starting transfers between devices, shards(): kept = kept + lax.ppermute(sent, 'core', swap)  21.7 us
    pallas_call x1, Pallas kernels, project(): pl.pallas_call(functools.partial(project_kernel, count, keys), out_shape=...  20.8 us
    ppermute x14, waiting for transfers between devices, ring(): got[key] = lax.ppermute(x, 'band', ways[way])  11.4 us
    dot_general x16, matrix products, dot(): lax.dot_general(left, piece, (((1,), (1,)), ((), ())), preferred_element_...  5.72 us
    unnamed x44, local copies, waits for them, and re-layouts  3.59 us
    ppermute x1, starting transfers between devices, shards(): other_margin = lax.ppermute(margin, 'core', swap)  3.02 us
  transfers between devices with their start and end apart: 17, of which 9 were waited for; matrix products, arithmetic and copies ran while one was open for 4% of the time, Pallas kernels for 0%

profile of v1, /device:TPU:513, one launch (start us, length us, event | category | flops | bytes accessed | tf_op | source)
XLA Modules:
  0.0 135.0 jit_solution(6488060445252340311)
XLA Ops:
  0.6 1.2 negate_convert_fusion
  1.9 4.5 %collective-permute-start.1 = (bf16[48,3072]{1,0:T(8,128)(2,1)S(1)}, bf16[48,3072]{1,0:T(8,128)(2,1)S(1)}, u32[]{:S(2)}, u32[]{:S(2)}) collective-permute-start(bf16[48,3072]{1,0:T(8,128)(2,1)S(1)} %get-tuple-element.2.refs_7_), channel_id=1, source_target_pairs={{0,7},{1,0},{2,1},{3,2},{4,3},{5,4},{6,5},{7,6},{8,15},{9,8},{10,9... | collective-permute-start | bytes 884744 | tf_op jit(solution)/shard_map/ppermute | solution.py:273
  6.4 2.7 %collective-permute-start.3 = (bf16[48,3072]{1,0:T(8,128)(2,1)S(1)}, bf16[48,3072]{1,0:T(8,128)(2,1)S(1)}, u32[]{:S(2)}, u32[]{:S(2)}) collective-permute-start(bf16[48,3072]{1,0:T(8,128)(2,1)S(1)} %get-tuple-element.3.refs_6_), channel_id=1, source_target_pairs={{0,7},{1,0},{2,1},{3,2},{4,3},{5,4},{6,5},{7,6},{8,15},{9,8},{10,9... | collective-permute-start | bytes 884744 | tf_op jit(solution)/shard_map/ppermute | solution.py:273
  9.2 0.4 fusion.2
  9.6 0.4 convolution_dynamic-update-slice_fusion.14
  10.0 6.4 %collective-permute-done.refs_8_ = bf16[48,3072]{1,0:T(8,128)(2,1)S(1)} collective-permute-done((bf16[48,3072]{1,0:T(8,128)(2,1)S(1)}, bf16[48,3072]{1,0:T(8,128)(2,1)S(1)}, u32[]{:S(2)}, u32[]{:S(2)}) %collective-permute-start) | collective-permute-done | bytes 294944 | tf_op jit(solution)/shard_map/ppermute | solution.py:273
  16.3 0.4 convolution_dynamic-update-slice_fusion.13
  16.7 0.4 copy-done.7
  17.1 3.0 %collective-permute-start.5 = (bf16[48,3072]{1,0:T(8,128)(2,1)S(1)}, bf16[48,3072]{1,0:T(8,128)(2,1)S(1)}, u32[]{:S(2)}, u32[]{:S(2)}) collective-permute-start(bf16[48,3072]{1,0:T(8,128)(2,1)S(1)} %collective-permute-done.1.refs_9_), channel_id=1, source_target_pairs={{0,7},{1,0},{2,1},{3,2},{4,3},{5,4},{6,5},{7,6},{8,15},{9,8},{10,9... | collective-permute-start | bytes 884744 | tf_op jit(solution)/shard_map/ppermute | solution.py:273
  20.1 0.4 convolution_dynamic-update-slice_fusion.12
  20.4 0.0 copy-done.5
  20.5 0.1 collective-permute-start.6
  20.6 0.4 convolution_dynamic-update-slice_fusion.11
  21.0 0.2 copy-done.6
  21.2 3.1 %collective-permute-start.7 = (bf16[48,3072]{1,0:T(8,128)(2,1)S(1)}, bf16[48,3072]{1,0:T(8,128)(2,1)S(1)}, u32[]{:S(2)}, u32[]{:S(2)}) collective-permute-start(bf16[48,3072]{1,0:T(8,128)(2,1)S(1)} %collective-permute-done.3.refs_11_), channel_id=1, source_target_pairs={{0,7},{1,0},{2,1},{3,2},{4,3},{5,4},{6,5},{7,6},{8,15},{9,8},{10,9... | collective-permute-start | bytes 884744 | tf_op jit(solution)/shard_map/ppermute | solution.py:273
  24.3 0.4 convolution_dynamic-update-slice_fusion.10
  24.7 0.0 copy-done.8
  24.7 0.1 collective-permute-start.8
  24.8 0.4 convolution_dynamic-update-slice_fusion.9
  25.2 0.2 copy-done.9
  25.4 2.6 %collective-permute-start.9 = (bf16[48,3072]{1,0:T(8,128)(2,1)S(1)}, bf16[48,3072]{1,0:T(8,128)(2,1)S(1)}, u32[]{:S(2)}, u32[]{:S(2)}) collective-permute-start(bf16[48,3072]{1,0:T(8,128)(2,1)S(1)} %collective-permute-done.5.refs_13_), channel_id=1, source_target_pairs={{0,7},{1,0},{2,1},{3,2},{4,3},{5,4},{6,5},{7,6},{8,15},{9,8},{10,9... | collective-permute-start | bytes 884744 | tf_op jit(solution)/shard_map/ppermute | solution.py:273
  28.0 0.4 convolution_dynamic-update-slice_fusion.8
  28.4 0.9 collective-permute-done.6.refs_14_
  29.3 0.4 convolution_dynamic-update-slice_fusion.7
  29.7 0.3 copy-done.11
  30.0 1.1 collective-permute-done.7.refs_15_
  31.1 3.4 %collective-permute-start.11 = (bf16[48,3072]{1,0:T(8,128)(2,1)S(1)}, bf16[48,3072]{1,0:T(8,128)(2,1)S(1)}, u32[]{:S(2)}, u32[]{:S(2)}) collective-permute-start(bf16[48,3072]{1,0:T(8,128)(2,1)S(1)} %collective-permute-done.7.refs_15_), channel_id=1, source_target_pairs={{0,7},{1,0},{2,1},{3,2},{4,3},{5,4},{6,5},{7,6},{8,15},{9,8},{10,9... | collective-permute-start | bytes 884744 | tf_op jit(solution)/shard_map/ppermute | solution.py:273
  34.5 0.4 convolution_dynamic-update-slice_fusion.6
  34.9 0.0 copy-done.12
  34.9 0.7 collective-permute-done.8.refs_16_
  35.6 0.4 convolution_dynamic-update-slice_fusion.5
  36.0 0.3 copy-done.13
  36.3 0.1 collective-permute-done.9.refs_17_
  36.4 3.1 %collective-permute-start.13 = (bf16[48,3072]{1,0:T(8,128)(2,1)S(1)}, bf16[48,3072]{1,0:T(8,128)(2,1)S(1)}, u32[]{:S(2)}, u32[]{:S(2)}) collective-permute-start(bf16[48,3072]{1,0:T(8,128)(2,1)S(1)} %collective-permute-done.9.refs_17_), channel_id=1, source_target_pairs={{0,7},{1,0},{2,1},{3,2},{4,3},{5,4},{6,5},{7,6},{8,15},{9,8},{10,9... | collective-permute-start | bytes 884744 | tf_op jit(solution)/shard_map/ppermute | solution.py:273
  39.5 0.4 convolution_dynamic-update-slice_fusion.4
  39.9 0.0 copy-done.14
  39.9 0.6 collective-permute-done.10.refs_18_
  40.5 0.4 convolution_dynamic-update-slice_fusion.3
  40.8 0.3 copy-done.15
  41.2 0.4 convolution_dynamic-update-slice_fusion.2
  41.6 0.3 copy-done.16
  41.9 1.7 %collective-permute-done.12.refs_20_ = bf16[48,3072]{1,0:T(8,128)(2,1)S(1)} collective-permute-done((bf16[48,3072]{1,0:T(8,128)(2,1)S(1)}, bf16[48,3072]{1,0:T(8,128)(2,1)S(1)}, u32[]{:S(2)}, u32[]{:S(2)}) %collective-permute-start.12) | collective-permute-done | bytes 294944 | tf_op jit(solution)/shard_map/ppermute | solution.py:273
  43.6 0.4 convolution_dynamic-update-slice_fusion.1
  44.0 0.3 copy-done.17
  44.3 0.4 convolution_dynamic-update-slice_fusion
  44.7 0.3 copy-done.18
  45.1 0.2 constant_dynamic-slice_fusion
  45.2 21.7 %collective-permute-start.14 = (f32[64,768]{0,1:T(8,128)S(1)}, f32[64,768]{0,1:T(8,128)S(1)}, u32[]{:S(2)}, u32[]{:S(2)}) collective-permute-start(f32[64,768]{0,1:T(8,128)S(1)} %constant_dynamic-slice_fusion), channel_id=1, source_target_pairs={{0,8},{8,0},{1,9},{9,1},{2,10},{10,2},{3,11},{11,3},{4,12},{12,4},... | collective-permute-start | bytes 589832 | tf_op jit(solution)/shard_map/ppermute | solution.py:313
  66.9 1.3 collective-permute-done.14
  68.3 0.2 add_convert_fusion
  68.5 0.1 fusion.6
  68.6 0.1 copy.10
  68.7 0.1 copy.11
  68.7 0.1 copy.12
  68.8 0.1 copy.13
  69.0 23.4 %all_to_all.10 = bf16[8,48,768]{2,1,0:T(8,128)(2,1)S(1)} all-to-all(bf16[8,48,768]{2,1,0:T(8,128)(2,1)S(1)} %broadcast_in_dim.10), channel_id=1, replica_groups=mesh['img'=2,'y'=8,'core'=2,'band'=8] {'y'}, dimensions={0} | all-to-all | bytes 1179648 | tf_op jit(solution)/shard_map/all_to_all | solution.py:286
  92.4 0.1 convert_reduce_fusion
  92.6 16.2 %all_to_all.11.refs_2_ = bf16[8,48,512]{2,1,0:T(8,128)(2,1)S(1)} all-to-all(bf16[8,48,512]{2,1,0:T(8,128)(2,1)S(1)} %broadcast_in_dim.11), channel_id=1, replica_groups=mesh['img'=2,'y'=8,'core'=2,'band'=8] {'band'}, dimensions={0} | all-to-all | bytes 786432 | tf_op jit(solution)/shard_map/all_to_all | solution.py:286
  108.8 3.0 %collective-permute-start.15 = (bf16[8,48,512]{2,1,0:T(8,128)(2,1)S(1)}, bf16[8,48,512]{2,1,0:T(8,128)(2,1)S(1)}, u32[]{:S(2)}, u32[]{:S(2)}) collective-permute-start(bf16[8,48,512]{2,1,0:T(8,128)(2,1)S(1)} %all_to_all.11.refs_2_), channel_id=1, source_target_pairs={{0,8},{8,0},{1,9},{9,1},{2,10},{10,2},{3,11},{11,3},{4,12},{12,4},... | collective-permute-start | bytes 1179656 | tf_op jit(solution)/shard_map/ppermute | solution.py:327
  111.8 0.1 collective-permute-start.16
  112.0 1.2 collective-permute-done.16.refs_5_
  113.2 0.6 copy-done.21
  113.8 0.1 copy-done.4
  114.0 20.8 %project.1 = (bf16[96,3072]{1,0:T(8,128)(2,1)}, bf16[32,3072]{1,0:T(8,128)(2,1)}) custom-call(s32[1]{0:T(128)} %bitcast.refs_0_, s32[1]{0:T(128)} %bitcast.1.refs_1_, bf16[8,48,512]{2,1,0:T(8,128)(2,1)} %copy-done.1, bf16[8,48,512]{2,1,0:T(8,128)(2,1)} %copy-done.4, f32[16,768]{1,0:T(8,128)} %copy-done.19, f32[16,768]{1,0:T(8,128)} %copy-done.21, ...), custom_call_target="tpu_custom_call" | custom-call | tf_op jit(solution)/shard_map/project/pallas_call | solution.py:229
  (54 shorter events, 0.3 us)
Async XLA Ops:
  1.8 7.3 %copy-start = (bf16[96,3072]{1,0:T(8,128)(2,1)S(1)}, bf16[96,3072]{1,0:T(8,128)(2,1)}, u32[]{:S(2)}) copy-start(bf16[96,3072]{1,0:T(8,128)(2,1)} %param.3) | copy-start | bytes 1769476
  1.9 7.2 %copy-start.2 = (bf16[48,3072]{1,0:T(8,128)(2,1)}, bf16[48,3072]{1,0:T(8,128)(2,1)S(1)}, u32[]{:S(2)}) copy-start(bf16[48,3072]{1,0:T(8,128)(2,1)S(1)} %get-tuple-element.2.refs_7_) | copy-start | bytes 884740
  1.9 7.2 %copy-start.3 = (bf16[48,3072]{1,0:T(8,128)(2,1)}, bf16[48,3072]{1,0:T(8,128)(2,1)S(1)}, u32[]{:S(2)}) copy-start(bf16[48,3072]{1,0:T(8,128)(2,1)S(1)} %get-tuple-element.3.refs_6_) | copy-start | bytes 884740
  1.9 15.2 %collective-permute-start.1 = (bf16[48,3072]{1,0:T(8,128)(2,1)S(1)}, bf16[48,3072]{1,0:T(8,128)(2,1)S(1)}, u32[]{:S(2)}, u32[]{:S(2)}) collective-permute-start(bf16[48,3072]{1,0:T(8,128)(2,1)S(1)} %get-tuple-element.2.refs_7_), channel_id=1, source_target_pairs={{0,7},{1,0},{2,1},{3,2},{4,3},{5,4},{6,5},{7,6},{8,15},{9,8},{10,9... | collective-permute-start | bytes 884744 | tf_op jit(solution)/shard_map/ppermute | solution.py:273
  6.4 14.1 %collective-permute-start.2 = (bf16[48,3072]{1,0:T(8,128)(2,1)S(1)}, bf16[48,3072]{1,0:T(8,128)(2,1)S(1)}, u32[]{:S(2)}, u32[]{:S(2)}) collective-permute-start(bf16[48,3072]{1,0:T(8,128)(2,1)S(1)} %get-tuple-element.2.refs_7_), channel_id=1, source_target_pairs={{0,1},{1,2},{2,3},{3,4},{4,5},{5,6},{6,7},{7,0},{8,9},{9,10},{10,1... | collective-permute-start | bytes 884744 | tf_op jit(solution)/shard_map/ppermute | solution.py:273
  6.4 2.8 %copy-start.20 = (bf16[32,3072]{1,0:T(8,128)(2,1)S(1)}, bf16[32,3072]{1,0:T(8,128)(2,1)}, u32[]{:S(2)}) copy-start(bf16[32,3072]{1,0:T(8,128)(2,1)} %param.5) | copy-start | bytes 589828
  6.4 9.9 %collective-permute-start = (bf16[48,3072]{1,0:T(8,128)(2,1)S(1)}, bf16[48,3072]{1,0:T(8,128)(2,1)S(1)}, u32[]{:S(2)}, u32[]{:S(2)}) collective-permute-start(bf16[48,3072]{1,0:T(8,128)(2,1)S(1)} %get-tuple-element.3.refs_6_), channel_id=1, source_target_pairs={{0,1},{1,2},{2,3},{3,4},{4,5},{5,6},{6,7},{7,0},{8,9},{9,10},{10,1... | collective-permute-start | bytes 884744 | tf_op jit(solution)/shard_map/ppermute | solution.py:273
  6.4 14.8 %collective-permute-start.3 = (bf16[48,3072]{1,0:T(8,128)(2,1)S(1)}, bf16[48,3072]{1,0:T(8,128)(2,1)S(1)}, u32[]{:S(2)}, u32[]{:S(2)}) collective-permute-start(bf16[48,3072]{1,0:T(8,128)(2,1)S(1)} %get-tuple-element.3.refs_6_), channel_id=1, source_target_pairs={{0,7},{1,0},{2,1},{3,2},{4,3},{5,4},{6,5},{7,6},{8,15},{9,8},{10,9... | collective-permute-start | bytes 884744 | tf_op jit(solution)/shard_map/ppermute | solution.py:273
  16.3 0.7 copy-start.7
  16.3 8.3 %collective-permute-start.4 = (bf16[48,3072]{1,0:T(8,128)(2,1)S(1)}, bf16[48,3072]{1,0:T(8,128)(2,1)S(1)}, u32[]{:S(2)}, u32[]{:S(2)}) collective-permute-start(bf16[48,3072]{1,0:T(8,128)(2,1)S(1)} %collective-permute-done.refs_8_), channel_id=1, source_target_pairs={{0,1},{1,2},{2,3},{3,4},{4,5},{5,6},{6,7},{7,0},{8,9},{9,10},{10,1... | collective-permute-start | bytes 884744 | tf_op jit(solution)/shard_map/ppermute | solution.py:273
  17.1 3.3 %copy-start.5 = (bf16[48,3072]{1,0:T(8,128)(2,1)}, bf16[48,3072]{1,0:T(8,128)(2,1)S(1)}, u32[]{:S(2)}) copy-start(bf16[48,3072]{1,0:T(8,128)(2,1)S(1)} %collective-permute-done.1.refs_9_) | copy-start | bytes 884740
  17.1 8.3 %collective-permute-start.5 = (bf16[48,3072]{1,0:T(8,128)(2,1)S(1)}, bf16[48,3072]{1,0:T(8,128)(2,1)S(1)}, u32[]{:S(2)}, u32[]{:S(2)}) collective-permute-start(bf16[48,3072]{1,0:T(8,128)(2,1)S(1)} %collective-permute-done.1.refs_9_), channel_id=1, source_target_pairs={{0,7},{1,0},{2,1},{3,2},{4,3},{5,4},{6,5},{7,6},{8,15},{9,8},{10,9... | collective-permute-start | bytes 884744 | tf_op jit(solution)/shard_map/ppermute | solution.py:273
  20.5 0.7 copy-start.6
  20.5 8.8 %collective-permute-start.6 = (bf16[48,3072]{1,0:T(8,128)(2,1)S(1)}, bf16[48,3072]{1,0:T(8,128)(2,1)S(1)}, u32[]{:S(2)}, u32[]{:S(2)}) collective-permute-start(bf16[48,3072]{1,0:T(8,128)(2,1)S(1)} %collective-permute-done.2.refs_10_), channel_id=1, source_target_pairs={{0,1},{1,2},{2,3},{3,4},{4,5},{5,6},{6,7},{7,0},{8,9},{9,10},{10,1... | collective-permute-start | bytes 884744 | tf_op jit(solution)/shard_map/ppermute | solution.py:273
  21.2 3.5 %copy-start.8 = (bf16[48,3072]{1,0:T(8,128)(2,1)}, bf16[48,3072]{1,0:T(8,128)(2,1)S(1)}, u32[]{:S(2)}) copy-start(bf16[48,3072]{1,0:T(8,128)(2,1)S(1)} %collective-permute-done.3.refs_11_) | copy-start | bytes 884740
  21.2 9.9 %collective-permute-start.7 = (bf16[48,3072]{1,0:T(8,128)(2,1)S(1)}, bf16[48,3072]{1,0:T(8,128)(2,1)S(1)}, u32[]{:S(2)}, u32[]{:S(2)}) collective-permute-start(bf16[48,3072]{1,0:T(8,128)(2,1)S(1)} %collective-permute-done.3.refs_11_), channel_id=1, source_target_pairs={{0,7},{1,0},{2,1},{3,2},{4,3},{5,4},{6,5},{7,6},{8,15},{9,8},{10,9... | collective-permute-start | bytes 884744 | tf_op jit(solution)/shard_map/ppermute | solution.py:273
  24.7 0.7 copy-start.9
  24.7 10.9 %collective-permute-start.8 = (bf16[48,3072]{1,0:T(8,128)(2,1)S(1)}, bf16[48,3072]{1,0:T(8,128)(2,1)S(1)}, u32[]{:S(2)}, u32[]{:S(2)}) collective-permute-start(bf16[48,3072]{1,0:T(8,128)(2,1)S(1)} %collective-permute-done.4.refs_12_), channel_id=1, source_target_pairs={{0,1},{1,2},{2,3},{3,4},{4,5},{5,6},{6,7},{7,0},{8,9},{9,10},{10,1... | collective-permute-start | bytes 884744 | tf_op jit(solution)/shard_map/ppermute | solution.py:273
  25.4 3.0 %copy-start.10 = (bf16[48,3072]{1,0:T(8,128)(2,1)}, bf16[48,3072]{1,0:T(8,128)(2,1)S(1)}, u32[]{:S(2)}) copy-start(bf16[48,3072]{1,0:T(8,128)(2,1)S(1)} %collective-permute-done.5.refs_13_) | copy-start | bytes 884740
  25.4 11.0 %collective-permute-start.9 = (bf16[48,3072]{1,0:T(8,128)(2,1)S(1)}, bf16[48,3072]{1,0:T(8,128)(2,1)S(1)}, u32[]{:S(2)}, u32[]{:S(2)}) collective-permute-start(bf16[48,3072]{1,0:T(8,128)(2,1)S(1)} %collective-permute-done.5.refs_13_), channel_id=1, source_target_pairs={{0,7},{1,0},{2,1},{3,2},{4,3},{5,4},{6,5},{7,6},{8,15},{9,8},{10,9... | collective-permute-start | bytes 884744 | tf_op jit(solution)/shard_map/ppermute | solution.py:273
  29.3 0.7 copy-start.11
  29.3 11.2 %collective-permute-start.10 = (bf16[48,3072]{1,0:T(8,128)(2,1)S(1)}, bf16[48,3072]{1,0:T(8,128)(2,1)S(1)}, u32[]{:S(2)}, u32[]{:S(2)}) collective-permute-start(bf16[48,3072]{1,0:T(8,128)(2,1)S(1)} %collective-permute-done.6.refs_14_), channel_id=1, source_target_pairs={{0,1},{1,2},{2,3},{3,4},{4,5},{5,6},{6,7},{7,0},{8,9},{9,10},{10,1... | collective-permute-start | bytes 884744 | tf_op jit(solution)/shard_map/ppermute | solution.py:273
  31.1 3.8 %copy-start.12 = (bf16[48,3072]{1,0:T(8,128)(2,1)}, bf16[48,3072]{1,0:T(8,128)(2,1)S(1)}, u32[]{:S(2)}) copy-start(bf16[48,3072]{1,0:T(8,128)(2,1)S(1)} %collective-permute-done.7.refs_15_) | copy-start | bytes 884740
  31.1 10.1 %collective-permute-start.11 = (bf16[48,3072]{1,0:T(8,128)(2,1)S(1)}, bf16[48,3072]{1,0:T(8,128)(2,1)S(1)}, u32[]{:S(2)}, u32[]{:S(2)}) collective-permute-start(bf16[48,3072]{1,0:T(8,128)(2,1)S(1)} %collective-permute-done.7.refs_15_), channel_id=1, source_target_pairs={{0,7},{1,0},{2,1},{3,2},{4,3},{5,4},{6,5},{7,6},{8,15},{9,8},{10,9... | collective-permute-start | bytes 884744 | tf_op jit(solution)/shard_map/ppermute | solution.py:273
  35.6 0.7 copy-start.13
  35.6 8.0 %collective-permute-start.12 = (bf16[48,3072]{1,0:T(8,128)(2,1)S(1)}, bf16[48,3072]{1,0:T(8,128)(2,1)S(1)}, u32[]{:S(2)}, u32[]{:S(2)}) collective-permute-start(bf16[48,3072]{1,0:T(8,128)(2,1)S(1)} %collective-permute-done.8.refs_16_), channel_id=1, source_target_pairs={{0,1},{1,2},{2,3},{3,4},{4,5},{5,6},{6,7},{7,0},{8,9},{9,10},{10,1... | collective-permute-start | bytes 884744 | tf_op jit(solution)/shard_map/ppermute | solution.py:273
  36.4 3.5 %copy-start.14 = (bf16[48,3072]{1,0:T(8,128)(2,1)}, bf16[48,3072]{1,0:T(8,128)(2,1)S(1)}, u32[]{:S(2)}) copy-start(bf16[48,3072]{1,0:T(8,128)(2,1)S(1)} %collective-permute-done.9.refs_17_) | copy-start | bytes 884740
  36.4 8.0 %collective-permute-start.13 = (bf16[48,3072]{1,0:T(8,128)(2,1)S(1)}, bf16[48,3072]{1,0:T(8,128)(2,1)S(1)}, u32[]{:S(2)}, u32[]{:S(2)}) collective-permute-start(bf16[48,3072]{1,0:T(8,128)(2,1)S(1)} %collective-permute-done.9.refs_17_), channel_id=1, source_target_pairs={{0,7},{1,0},{2,1},{3,2},{4,3},{5,4},{6,5},{7,6},{8,15},{9,8},{10,9... | collective-permute-start | bytes 884744 | tf_op jit(solution)/shard_map/ppermute | solution.py:273
  40.5 0.7 copy-start.15
  41.2 0.7 copy-start.16
  43.6 0.7 copy-start.17
  44.3 0.7 copy-start.18
  45.2 23.1 %collective-permute-start.14 = (f32[64,768]{0,1:T(8,128)S(1)}, f32[64,768]{0,1:T(8,128)S(1)}, u32[]{:S(2)}, u32[]{:S(2)}) collective-permute-start(f32[64,768]{0,1:T(8,128)S(1)} %constant_dynamic-slice_fusion), channel_id=1, source_target_pairs={{0,8},{8,0},{1,9},{9,1},{2,10},{10,2},{3,11},{11,3},{4,12},{12,4},... | collective-permute-start | bytes 589832 | tf_op jit(solution)/shard_map/ppermute | solution.py:313
  108.8 4.5 %copy-start.1 = (bf16[8,48,512]{2,1,0:T(8,128)(2,1)}, bf16[8,48,512]{2,1,0:T(8,128)(2,1)S(1)}, u32[]{:S(2)}) copy-start(bf16[8,48,512]{2,1,0:T(8,128)(2,1)S(1)} %all_to_all.11.refs_2_) | copy-start | bytes 1179652
  108.8 4.4 %collective-permute-start.15 = (bf16[8,48,512]{2,1,0:T(8,128)(2,1)S(1)}, bf16[8,48,512]{2,1,0:T(8,128)(2,1)S(1)}, u32[]{:S(2)}, u32[]{:S(2)}) collective-permute-start(bf16[8,48,512]{2,1,0:T(8,128)(2,1)S(1)} %all_to_all.11.refs_2_), channel_id=1, source_target_pairs={{0,8},{8,0},{1,9},{9,1},{2,10},{10,2},{3,11},{11,3},{4,12},{12,4},... | collective-permute-start | bytes 1179656 | tf_op jit(solution)/shard_map/ppermute | solution.py:327
  111.8 1.4 %copy-start.19 = (f32[16,768]{1,0:T(8,128)}, f32[16,768]{1,0:T(8,128)S(1)}, u32[]{:S(2)}) copy-start(f32[16,768]{1,0:T(8,128)S(1)} %pad_maximum_fusion.1.refs_4_) | copy-start | bytes 147460
  111.8 1.4 %collective-permute-start.16 = (f32[16,768]{1,0:T(8,128)S(1)}, f32[16,768]{1,0:T(8,128)S(1)}, u32[]{:S(2)}, u32[]{:S(2)}) collective-permute-start(f32[16,768]{1,0:T(8,128)S(1)} %pad_maximum_fusion.1.refs_4_), channel_id=1, source_target_pairs={{0,8},{8,0},{1,9},{9,1},{2,10},{10,2},{3,11},{11,3},{4,12},{12,4},... | collective-permute-start | bytes 147464 | tf_op jit(solution)/shard_map/ppermute | solution.py:331
  113.2 0.6 copy-start.21
  113.2 0.8 copy-start.4

commit v2 on v1

--- a/solution.py
+++ b/solution.py
@@ -18,14 +18,6 @@
 def split(a):
     hi = a.astype(jnp.bfloat16)
     return hi, (a - hi.astype(jnp.float32)).astype(jnp.bfloat16)
-
-
-def dot3(a, b, dims):
-    (ah, al), (bh, bl) = a, b
-    dot = functools.partial(
-        lax.dot_general, dimension_numbers=(dims, ((), ())), preferred_element_type=jnp.float32
-    )
-    return dot(ah, bh) + (dot(ah, bl) + dot(al, bh))
 
 
 def dot1(a, b, dims):
@@ -145,7 +137,7 @@
             a[them, :] = a[them, :] - dot1(factor, r, rows_of)
         here, after = block(b), block(jnp.minimum(b + 1, blocks - 1))
         g = g_ref[...]
-        r_ref[...] = dot3(split(g), split(a[here, :]), ((1,), (0,)))
+        r_ref[...] = dot2(g, a[here, :], ((1,), (0,)))
         factor = r_ref[:, after]
         d_ref[...] = a[after, after] - dot1(factor, factor, rows_of)
         r_ref[:, here] = g

time: 135 us -> 135 us (level)
  no operation moved by 1% of the time
where the time goes in v2:
time: 135 us
  starting transfers between devices  47.5 us (35%)
  blocking collectives  39.6 us (29%)
  Pallas kernels  20.7 us (15%)
  waiting for transfers between devices  14 us (10%)
  matrix products  5.72 us (4%)
  local copies, waits for them, and re-layouts  4.43 us (3%)
  other arithmetic  1.49 us (1%)
  between operations  1.35 us (1%)
    all_to_all x2, blocking collectives, to_all(): lax.all_to_all(jnp.broadcast_to(shard[None], (count, *shard.shape)), axis...  39.6 us
    ppermute x14, starting transfers between devices, ring(): got[key] = lax.ppermute(x, 'band', ways[way])  22.7 us
    ppermute x1, starting transfers between devices, shards(): kept = kept + lax.ppermute(sent, 'core', swap)  21.7 us
    pallas_call x1, Pallas kernels, project(): pl.pallas_call(functools.partial(project_kernel, count, keys), out_shape=...  20.7 us
    ppermute x14, waiting for transfers between devices, ring(): got[key] = lax.ppermute(x, 'band', ways[way])  11.4 us
    dot_general x16, matrix products, dot(): lax.dot_general(left, piece, (((1,), (1,)), ((), ())), preferred_element_...  5.72 us
    unnamed x44, local copies, waits for them, and re-layouts  3.59 us
    ppermute x1, starting transfers between devices, shards(): other_margin = lax.ppermute(margin, 'core', swap)  3.02 us
  transfers between devices with their start and end apart: 17, of which 9 were waited for; matrix products, arithmetic and copies ran while one was open for 4% of the time, Pallas kernels for 0%

profile of v2, /device:TPU:513, one launch (start us, length us, event | category | flops | bytes accessed | tf_op | source)
XLA Modules:
  0.0 134.9 jit_solution(16032874653626637668)
XLA Ops:
  0.6 1.2 negate_convert_fusion
  1.9 4.5 %collective-permute-start.1 = (bf16[48,3072]{1,0:T(8,128)(2,1)S(1)}, bf16[48,3072]{1,0:T(8,128)(2,1)S(1)}, u32[]{:S(2)}, u32[]{:S(2)}) collective-permute-start(bf16[48,3072]{1,0:T(8,128)(2,1)S(1)} %get-tuple-element.2.refs_7_), channel_id=1, source_target_pairs={{0,7},{1,0},{2,1},{3,2},{4,3},{5,4},{6,5},{7,6},{8,15},{9,8},{10,9... | collective-permute-start | bytes 884744 | tf_op jit(solution)/shard_map/ppermute | solution.py:265
  6.4 2.7 %collective-permute-start.3 = (bf16[48,3072]{1,0:T(8,128)(2,1)S(1)}, bf16[48,3072]{1,0:T(8,128)(2,1)S(1)}, u32[]{:S(2)}, u32[]{:S(2)}) collective-permute-start(bf16[48,3072]{1,0:T(8,128)(2,1)S(1)} %get-tuple-element.3.refs_6_), channel_id=1, source_target_pairs={{0,7},{1,0},{2,1},{3,2},{4,3},{5,4},{6,5},{7,6},{8,15},{9,8},{10,9... | collective-permute-start | bytes 884744 | tf_op jit(solution)/shard_map/ppermute | solution.py:265
  9.2 0.4 fusion.2
  9.6 0.4 convolution_dynamic-update-slice_fusion.14
  10.0 6.4 %collective-permute-done.refs_8_ = bf16[48,3072]{1,0:T(8,128)(2,1)S(1)} collective-permute-done((bf16[48,3072]{1,0:T(8,128)(2,1)S(1)}, bf16[48,3072]{1,0:T(8,128)(2,1)S(1)}, u32[]{:S(2)}, u32[]{:S(2)}) %collective-permute-start) | collective-permute-done | bytes 294944 | tf_op jit(solution)/shard_map/ppermute | solution.py:265
  16.3 0.4 convolution_dynamic-update-slice_fusion.13
  16.7 0.4 copy-done.7
  17.1 3.0 %collective-permute-start.5 = (bf16[48,3072]{1,0:T(8,128)(2,1)S(1)}, bf16[48,3072]{1,0:T(8,128)(2,1)S(1)}, u32[]{:S(2)}, u32[]{:S(2)}) collective-permute-start(bf16[48,3072]{1,0:T(8,128)(2,1)S(1)} %collective-permute-done.1.refs_9_), channel_id=1, source_target_pairs={{0,7},{1,0},{2,1},{3,2},{4,3},{5,4},{6,5},{7,6},{8,15},{9,8},{10,9... | collective-permute-start | bytes 884744 | tf_op jit(solution)/shard_map/ppermute | solution.py:265
  20.1 0.4 convolution_dynamic-update-slice_fusion.12
  20.4 0.0 copy-done.5
  20.5 0.1 collective-permute-start.6
  20.6 0.4 convolution_dynamic-update-slice_fusion.11
  21.0 0.2 copy-done.6
  21.2 3.1 %collective-permute-start.7 = (bf16[48,3072]{1,0:T(8,128)(2,1)S(1)}, bf16[48,3072]{1,0:T(8,128)(2,1)S(1)}, u32[]{:S(2)}, u32[]{:S(2)}) collective-permute-start(bf16[48,3072]{1,0:T(8,128)(2,1)S(1)} %collective-permute-done.3.refs_11_), channel_id=1, source_target_pairs={{0,7},{1,0},{2,1},{3,2},{4,3},{5,4},{6,5},{7,6},{8,15},{9,8},{10,9... | collective-permute-start | bytes 884744 | tf_op jit(solution)/shard_map/ppermute | solution.py:265
  24.3 0.4 convolution_dynamic-update-slice_fusion.10
  24.7 0.0 copy-done.8
  24.7 0.1 collective-permute-start.8
  24.8 0.4 convolution_dynamic-update-slice_fusion.9
  25.2 0.2 copy-done.9
  25.4 2.6 %collective-permute-start.9 = (bf16[48,3072]{1,0:T(8,128)(2,1)S(1)}, bf16[48,3072]{1,0:T(8,128)(2,1)S(1)}, u32[]{:S(2)}, u32[]{:S(2)}) collective-permute-start(bf16[48,3072]{1,0:T(8,128)(2,1)S(1)} %collective-permute-done.5.refs_13_), channel_id=1, source_target_pairs={{0,7},{1,0},{2,1},{3,2},{4,3},{5,4},{6,5},{7,6},{8,15},{9,8},{10,9... | collective-permute-start | bytes 884744 | tf_op jit(solution)/shard_map/ppermute | solution.py:265
  28.0 0.4 convolution_dynamic-update-slice_fusion.8
  28.4 0.9 collective-permute-done.6.refs_14_
  29.3 0.4 convolution_dynamic-update-slice_fusion.7
  29.7 0.3 copy-done.11
  30.0 1.1 collective-permute-done.7.refs_15_
  31.1 3.4 %collective-permute-start.11 = (bf16[48,3072]{1,0:T(8,128)(2,1)S(1)}, bf16[48,3072]{1,0:T(8,128)(2,1)S(1)}, u32[]{:S(2)}, u32[]{:S(2)}) collective-permute-start(bf16[48,3072]{1,0:T(8,128)(2,1)S(1)} %collective-permute-done.7.refs_15_), channel_id=1, source_target_pairs={{0,7},{1,0},{2,1},{3,2},{4,3},{5,4},{6,5},{7,6},{8,15},{9,8},{10,9... | collective-permute-start | bytes 884744 | tf_op jit(solution)/shard_map/ppermute | solution.py:265
  34.5 0.4 convolution_dynamic-update-slice_fusion.6
  34.9 0.0 copy-done.12
  34.9 0.7 collective-permute-done.8.refs_16_
  35.6 0.4 convolution_dynamic-update-slice_fusion.5
  36.0 0.3 copy-done.13
  36.3 0.1 collective-permute-done.9.refs_17_
  36.4 3.1 %collective-permute-start.13 = (bf16[48,3072]{1,0:T(8,128)(2,1)S(1)}, bf16[48,3072]{1,0:T(8,128)(2,1)S(1)}, u32[]{:S(2)}, u32[]{:S(2)}) collective-permute-start(bf16[48,3072]{1,0:T(8,128)(2,1)S(1)} %collective-permute-done.9.refs_17_), channel_id=1, source_target_pairs={{0,7},{1,0},{2,1},{3,2},{4,3},{5,4},{6,5},{7,6},{8,15},{9,8},{10,9... | collective-permute-start | bytes 884744 | tf_op jit(solution)/shard_map/ppermute | solution.py:265
  39.5 0.4 convolution_dynamic-update-slice_fusion.4
  39.9 0.0 copy-done.14
  39.9 0.6 collective-permute-done.10.refs_18_
  40.5 0.4 convolution_dynamic-update-slice_fusion.3
  40.8 0.3 copy-done.15
  41.2 0.4 convolution_dynamic-update-slice_fusion.2
  41.6 0.3 copy-done.16
  41.9 1.7 %collective-permute-done.12.refs_20_ = bf16[48,3072]{1,0:T(8,128)(2,1)S(1)} collective-permute-done((bf16[48,3072]{1,0:T(8,128)(2,1)S(1)}, bf16[48,3072]{1,0:T(8,128)(2,1)S(1)}, u32[]{:S(2)}, u32[]{:S(2)}) %collective-permute-start.12) | collective-permute-done | bytes 294944 | tf_op jit(solution)/shard_map/ppermute | solution.py:265
  43.6 0.4 convolution_dynamic-update-slice_fusion.1
  44.0 0.3 copy-done.17
  44.3 0.4 convolution_dynamic-update-slice_fusion
  44.7 0.3 copy-done.18
  45.1 0.2 constant_dynamic-slice_fusion
  45.2 21.7 %collective-permute-start.14 = (f32[64,768]{0,1:T(8,128)S(1)}, f32[64,768]{0,1:T(8,128)S(1)}, u32[]{:S(2)}, u32[]{:S(2)}) collective-permute-start(f32[64,768]{0,1:T(8,128)S(1)} %constant_dynamic-slice_fusion), channel_id=1, source_target_pairs={{0,8},{8,0},{1,9},{9,1},{2,10},{10,2},{3,11},{11,3},{4,12},{12,4},... | collective-permute-start | bytes 589832 | tf_op jit(solution)/shard_map/ppermute | solution.py:305
  66.9 1.3 %collective-permute-done.14 = f32[64,768]{0,1:T(8,128)S(1)} collective-permute-done((f32[64,768]{0,1:T(8,128)S(1)}, f32[64,768]{0,1:T(8,128)S(1)}, u32[]{:S(2)}, u32[]{:S(2)}) %collective-permute-start.14) | collective-permute-done | bytes 196640 | tf_op jit(solution)/shard_map/ppermute | solution.py:305
  68.3 0.2 add_convert_fusion
  68.5 0.1 fusion.6
  68.6 0.1 copy.10
  68.7 0.1 copy.11
  68.7 0.1 copy.12
  68.8 0.1 copy.13
  69.0 23.4 %all_to_all.10 = bf16[8,48,768]{2,1,0:T(8,128)(2,1)S(1)} all-to-all(bf16[8,48,768]{2,1,0:T(8,128)(2,1)S(1)} %broadcast_in_dim.10), channel_id=1, replica_groups=mesh['img'=2,'y'=8,'core'=2,'band'=8] {'y'}, dimensions={0} | all-to-all | bytes 1179648 | tf_op jit(solution)/shard_map/all_to_all | solution.py:278
  92.4 0.1 convert_reduce_fusion
  92.6 16.2 %all_to_all.11.refs_2_ = bf16[8,48,512]{2,1,0:T(8,128)(2,1)S(1)} all-to-all(bf16[8,48,512]{2,1,0:T(8,128)(2,1)S(1)} %broadcast_in_dim.11), channel_id=1, replica_groups=mesh['img'=2,'y'=8,'core'=2,'band'=8] {'band'}, dimensions={0} | all-to-all | bytes 786432 | tf_op jit(solution)/shard_map/all_to_all | solution.py:278
  108.8 3.0 %collective-permute-start.15 = (bf16[8,48,512]{2,1,0:T(8,128)(2,1)S(1)}, bf16[8,48,512]{2,1,0:T(8,128)(2,1)S(1)}, u32[]{:S(2)}, u32[]{:S(2)}) collective-permute-start(bf16[8,48,512]{2,1,0:T(8,128)(2,1)S(1)} %all_to_all.11.refs_2_), channel_id=1, source_target_pairs={{0,8},{8,0},{1,9},{9,1},{2,10},{10,2},{3,11},{11,3},{4,12},{12,4},... | collective-permute-start | bytes 1179656 | tf_op jit(solution)/shard_map/ppermute | solution.py:319
  111.8 0.1 collective-permute-start.16
  112.0 1.2 collective-permute-done.16.refs_5_
  113.2 0.6 copy-done.21
  113.8 0.1 copy-done.4
  114.0 20.7 %project.1 = (bf16[96,3072]{1,0:T(8,128)(2,1)}, bf16[32,3072]{1,0:T(8,128)(2,1)}) custom-call(s32[1]{0:T(128)} %bitcast.refs_0_, s32[1]{0:T(128)} %bitcast.1.refs_1_, bf16[8,48,512]{2,1,0:T(8,128)(2,1)} %copy-done.1, bf16[8,48,512]{2,1,0:T(8,128)(2,1)} %copy-done.4, f32[16,768]{1,0:T(8,128)} %copy-done.19, f32[16,768]{1,0:T(8,128)} %copy-done.21, ...), custom_call_target="tpu_custom_call" | custom-call | tf_op jit(solution)/shard_map/project/pallas_call | solution.py:221
  (54 shorter events, 0.3 us)
Async XLA Ops:
  1.8 7.3 %copy-start = (bf16[96,3072]{1,0:T(8,128)(2,1)S(1)}, bf16[96,3072]{1,0:T(8,128)(2,1)}, u32[]{:S(2)}) copy-start(bf16[96,3072]{1,0:T(8,128)(2,1)} %param.3) | copy-start | bytes 1769476
  1.9 7.2 %copy-start.2 = (bf16[48,3072]{1,0:T(8,128)(2,1)}, bf16[48,3072]{1,0:T(8,128)(2,1)S(1)}, u32[]{:S(2)}) copy-start(bf16[48,3072]{1,0:T(8,128)(2,1)S(1)} %get-tuple-element.2.refs_7_) | copy-start | bytes 884740
  1.9 7.2 %copy-start.3 = (bf16[48,3072]{1,0:T(8,128)(2,1)}, bf16[48,3072]{1,0:T(8,128)(2,1)S(1)}, u32[]{:S(2)}) copy-start(bf16[48,3072]{1,0:T(8,128)(2,1)S(1)} %get-tuple-element.3.refs_6_) | copy-start | bytes 884740
  1.9 15.2 %collective-permute-start.1 = (bf16[48,3072]{1,0:T(8,128)(2,1)S(1)}, bf16[48,3072]{1,0:T(8,128)(2,1)S(1)}, u32[]{:S(2)}, u32[]{:S(2)}) collective-permute-start(bf16[48,3072]{1,0:T(8,128)(2,1)S(1)} %get-tuple-element.2.refs_7_), channel_id=1, source_target_pairs={{0,7},{1,0},{2,1},{3,2},{4,3},{5,4},{6,5},{7,6},{8,15},{9,8},{10,9... | collective-permute-start | bytes 884744 | tf_op jit(solution)/shard_map/ppermute | solution.py:265
  6.4 14.1 %collective-permute-start.2 = (bf16[48,3072]{1,0:T(8,128)(2,1)S(1)}, bf16[48,3072]{1,0:T(8,128)(2,1)S(1)}, u32[]{:S(2)}, u32[]{:S(2)}) collective-permute-start(bf16[48,3072]{1,0:T(8,128)(2,1)S(1)} %get-tuple-element.2.refs_7_), channel_id=1, source_target_pairs={{0,1},{1,2},{2,3},{3,4},{4,5},{5,6},{6,7},{7,0},{8,9},{9,10},{10,1... | collective-permute-start | bytes 884744 | tf_op jit(solution)/shard_map/ppermute | solution.py:265
  6.4 2.8 %copy-start.20 = (bf16[32,3072]{1,0:T(8,128)(2,1)S(1)}, bf16[32,3072]{1,0:T(8,128)(2,1)}, u32[]{:S(2)}) copy-start(bf16[32,3072]{1,0:T(8,128)(2,1)} %param.5) | copy-start | bytes 589828
  6.4 9.9 %collective-permute-start = (bf16[48,3072]{1,0:T(8,128)(2,1)S(1)}, bf16[48,3072]{1,0:T(8,128)(2,1)S(1)}, u32[]{:S(2)}, u32[]{:S(2)}) collective-permute-start(bf16[48,3072]{1,0:T(8,128)(2,1)S(1)} %get-tuple-element.3.refs_6_), channel_id=1, source_target_pairs={{0,1},{1,2},{2,3},{3,4},{4,5},{5,6},{6,7},{7,0},{8,9},{9,10},{10,1... | collective-permute-start | bytes 884744 | tf_op jit(solution)/shard_map/ppermute | solution.py:265
  6.4 14.8 %collective-permute-start.3 = (bf16[48,3072]{1,0:T(8,128)(2,1)S(1)}, bf16[48,3072]{1,0:T(8,128)(2,1)S(1)}, u32[]{:S(2)}, u32[]{:S(2)}) collective-permute-start(bf16[48,3072]{1,0:T(8,128)(2,1)S(1)} %get-tuple-element.3.refs_6_), channel_id=1, source_target_pairs={{0,7},{1,0},{2,1},{3,2},{4,3},{5,4},{6,5},{7,6},{8,15},{9,8},{10,9... | collective-permute-start | bytes 884744 | tf_op jit(solution)/shard_map/ppermute | solution.py:265
  16.3 0.7 copy-start.7
  16.3 8.3 %collective-permute-start.4 = (bf16[48,3072]{1,0:T(8,128)(2,1)S(1)}, bf16[48,3072]{1,0:T(8,128)(2,1)S(1)}, u32[]{:S(2)}, u32[]{:S(2)}) collective-permute-start(bf16[48,3072]{1,0:T(8,128)(2,1)S(1)} %collective-permute-done.refs_8_), channel_id=1, source_target_pairs={{0,1},{1,2},{2,3},{3,4},{4,5},{5,6},{6,7},{7,0},{8,9},{9,10},{10,1... | collective-permute-start | bytes 884744 | tf_op jit(solution)/shard_map/ppermute | solution.py:265
  17.1 3.3 %copy-start.5 = (bf16[48,3072]{1,0:T(8,128)(2,1)}, bf16[48,3072]{1,0:T(8,128)(2,1)S(1)}, u32[]{:S(2)}) copy-start(bf16[48,3072]{1,0:T(8,128)(2,1)S(1)} %collective-permute-done.1.refs_9_) | copy-start | bytes 884740
  17.1 8.3 %collective-permute-start.5 = (bf16[48,3072]{1,0:T(8,128)(2,1)S(1)}, bf16[48,3072]{1,0:T(8,128)(2,1)S(1)}, u32[]{:S(2)}, u32[]{:S(2)}) collective-permute-start(bf16[48,3072]{1,0:T(8,128)(2,1)S(1)} %collective-permute-done.1.refs_9_), channel_id=1, source_target_pairs={{0,7},{1,0},{2,1},{3,2},{4,3},{5,4},{6,5},{7,6},{8,15},{9,8},{10,9... | collective-permute-start | bytes 884744 | tf_op jit(solution)/shard_map/ppermute | solution.py:265
  20.5 0.7 copy-start.6
  20.5 8.8 %collective-permute-start.6 = (bf16[48,3072]{1,0:T(8,128)(2,1)S(1)}, bf16[48,3072]{1,0:T(8,128)(2,1)S(1)}, u32[]{:S(2)}, u32[]{:S(2)}) collective-permute-start(bf16[48,3072]{1,0:T(8,128)(2,1)S(1)} %collective-permute-done.2.refs_10_), channel_id=1, source_target_pairs={{0,1},{1,2},{2,3},{3,4},{4,5},{5,6},{6,7},{7,0},{8,9},{9,10},{10,1... | collective-permute-start | bytes 884744 | tf_op jit(solution)/shard_map/ppermute | solution.py:265
  21.2 3.5 %copy-start.8 = (bf16[48,3072]{1,0:T(8,128)(2,1)}, bf16[48,3072]{1,0:T(8,128)(2,1)S(1)}, u32[]{:S(2)}) copy-start(bf16[48,3072]{1,0:T(8,128)(2,1)S(1)} %collective-permute-done.3.refs_11_) | copy-start | bytes 884740
  21.2 9.9 %collective-permute-start.7 = (bf16[48,3072]{1,0:T(8,128)(2,1)S(1)}, bf16[48,3072]{1,0:T(8,128)(2,1)S(1)}, u32[]{:S(2)}, u32[]{:S(2)}) collective-permute-start(bf16[48,3072]{1,0:T(8,128)(2,1)S(1)} %collective-permute-done.3.refs_11_), channel_id=1, source_target_pairs={{0,7},{1,0},{2,1},{3,2},{4,3},{5,4},{6,5},{7,6},{8,15},{9,8},{10,9... | collective-permute-start | bytes 884744 | tf_op jit(solution)/shard_map/ppermute | solution.py:265
  24.7 0.7 copy-start.9
  24.7 10.9 %collective-permute-start.8 = (bf16[48,3072]{1,0:T(8,128)(2,1)S(1)}, bf16[48,3072]{1,0:T(8,128)(2,1)S(1)}, u32[]{:S(2)}, u32[]{:S(2)}) collective-permute-start(bf16[48,3072]{1,0:T(8,128)(2,1)S(1)} %collective-permute-done.4.refs_12_), channel_id=1, source_target_pairs={{0,1},{1,2},{2,3},{3,4},{4,5},{5,6},{6,7},{7,0},{8,9},{9,10},{10,1... | collective-permute-start | bytes 884744 | tf_op jit(solution)/shard_map/ppermute | solution.py:265
  25.4 3.0 %copy-start.10 = (bf16[48,3072]{1,0:T(8,128)(2,1)}, bf16[48,3072]{1,0:T(8,128)(2,1)S(1)}, u32[]{:S(2)}) copy-start(bf16[48,3072]{1,0:T(8,128)(2,1)S(1)} %collective-permute-done.5.refs_13_) | copy-start | bytes 884740
  25.4 11.0 %collective-permute-start.9 = (bf16[48,3072]{1,0:T(8,128)(2,1)S(1)}, bf16[48,3072]{1,0:T(8,128)(2,1)S(1)}, u32[]{:S(2)}, u32[]{:S(2)}) collective-permute-start(bf16[48,3072]{1,0:T(8,128)(2,1)S(1)} %collective-permute-done.5.refs_13_), channel_id=1, source_target_pairs={{0,7},{1,0},{2,1},{3,2},{4,3},{5,4},{6,5},{7,6},{8,15},{9,8},{10,9... | collective-permute-start | bytes 884744 | tf_op jit(solution)/shard_map/ppermute | solution.py:265
  29.3 0.7 copy-start.11
  29.3 11.2 %collective-permute-start.10 = (bf16[48,3072]{1,0:T(8,128)(2,1)S(1)}, bf16[48,3072]{1,0:T(8,128)(2,1)S(1)}, u32[]{:S(2)}, u32[]{:S(2)}) collective-permute-start(bf16[48,3072]{1,0:T(8,128)(2,1)S(1)} %collective-permute-done.6.refs_14_), channel_id=1, source_target_pairs={{0,1},{1,2},{2,3},{3,4},{4,5},{5,6},{6,7},{7,0},{8,9},{9,10},{10,1... | collective-permute-start | bytes 884744 | tf_op jit(solution)/shard_map/ppermute | solution.py:265
  31.1 3.8 %copy-start.12 = (bf16[48,3072]{1,0:T(8,128)(2,1)}, bf16[48,3072]{1,0:T(8,128)(2,1)S(1)}, u32[]{:S(2)}) copy-start(bf16[48,3072]{1,0:T(8,128)(2,1)S(1)} %collective-permute-done.7.refs_15_) | copy-start | bytes 884740
  31.1 10.1 %collective-permute-start.11 = (bf16[48,3072]{1,0:T(8,128)(2,1)S(1)}, bf16[48,3072]{1,0:T(8,128)(2,1)S(1)}, u32[]{:S(2)}, u32[]{:S(2)}) collective-permute-start(bf16[48,3072]{1,0:T(8,128)(2,1)S(1)} %collective-permute-done.7.refs_15_), channel_id=1, source_target_pairs={{0,7},{1,0},{2,1},{3,2},{4,3},{5,4},{6,5},{7,6},{8,15},{9,8},{10,9... | collective-permute-start | bytes 884744 | tf_op jit(solution)/shard_map/ppermute | solution.py:265
  35.6 0.7 copy-start.13
  35.6 8.0 %collective-permute-start.12 = (bf16[48,3072]{1,0:T(8,128)(2,1)S(1)}, bf16[48,3072]{1,0:T(8,128)(2,1)S(1)}, u32[]{:S(2)}, u32[]{:S(2)}) collective-permute-start(bf16[48,3072]{1,0:T(8,128)(2,1)S(1)} %collective-permute-done.8.refs_16_), channel_id=1, source_target_pairs={{0,1},{1,2},{2,3},{3,4},{4,5},{5,6},{6,7},{7,0},{8,9},{9,10},{10,1... | collective-permute-start | bytes 884744 | tf_op jit(solution)/shard_map/ppermute | solution.py:265
  36.4 3.5 %copy-start.14 = (bf16[48,3072]{1,0:T(8,128)(2,1)}, bf16[48,3072]{1,0:T(8,128)(2,1)S(1)}, u32[]{:S(2)}) copy-start(bf16[48,3072]{1,0:T(8,128)(2,1)S(1)} %collective-permute-done.9.refs_17_) | copy-start | bytes 884740
  36.4 8.0 %collective-permute-start.13 = (bf16[48,3072]{1,0:T(8,128)(2,1)S(1)}, bf16[48,3072]{1,0:T(8,128)(2,1)S(1)}, u32[]{:S(2)}, u32[]{:S(2)}) collective-permute-start(bf16[48,3072]{1,0:T(8,128)(2,1)S(1)} %collective-permute-done.9.refs_17_), channel_id=1, source_target_pairs={{0,7},{1,0},{2,1},{3,2},{4,3},{5,4},{6,5},{7,6},{8,15},{9,8},{10,9... | collective-permute-start | bytes 884744 | tf_op jit(solution)/shard_map/ppermute | solution.py:265
  40.5 0.7 copy-start.15
  41.2 0.7 copy-start.16
  43.6 0.7 copy-start.17
  44.3 0.7 copy-start.18
  45.2 23.1 %collective-permute-start.14 = (f32[64,768]{0,1:T(8,128)S(1)}, f32[64,768]{0,1:T(8,128)S(1)}, u32[]{:S(2)}, u32[]{:S(2)}) collective-permute-start(f32[64,768]{0,1:T(8,128)S(1)} %constant_dynamic-slice_fusion), channel_id=1, source_target_pairs={{0,8},{8,0},{1,9},{9,1},{2,10},{10,2},{3,11},{11,3},{4,12},{12,4},... | collective-permute-start | bytes 589832 | tf_op jit(solution)/shard_map/ppermute | solution.py:305
  108.8 4.5 %copy-start.1 = (bf16[8,48,512]{2,1,0:T(8,128)(2,1)}, bf16[8,48,512]{2,1,0:T(8,128)(2,1)S(1)}, u32[]{:S(2)}) copy-start(bf16[8,48,512]{2,1,0:T(8,128)(2,1)S(1)} %all_to_all.11.refs_2_) | copy-start | bytes 1179652
  108.8 4.4 %collective-permute-start.15 = (bf16[8,48,512]{2,1,0:T(8,128)(2,1)S(1)}, bf16[8,48,512]{2,1,0:T(8,128)(2,1)S(1)}, u32[]{:S(2)}, u32[]{:S(2)}) collective-permute-start(bf16[8,48,512]{2,1,0:T(8,128)(2,1)S(1)} %all_to_all.11.refs_2_), channel_id=1, source_target_pairs={{0,8},{8,0},{1,9},{9,1},{2,10},{10,2},{3,11},{11,3},{4,12},{12,4},... | collective-permute-start | bytes 1179656 | tf_op jit(solution)/shard_map/ppermute | solution.py:319
  111.8 1.4 %copy-start.19 = (f32[16,768]{1,0:T(8,128)}, f32[16,768]{1,0:T(8,128)S(1)}, u32[]{:S(2)}) copy-start(f32[16,768]{1,0:T(8,128)S(1)} %pad_maximum_fusion.1.refs_4_) | copy-start | bytes 147460
  111.8 1.4 %collective-permute-start.16 = (f32[16,768]{1,0:T(8,128)S(1)}, f32[16,768]{1,0:T(8,128)S(1)}, u32[]{:S(2)}, u32[]{:S(2)}) collective-permute-start(f32[16,768]{1,0:T(8,128)S(1)} %pad_maximum_fusion.1.refs_4_), channel_id=1, source_target_pairs={{0,8},{8,0},{1,9},{9,1},{2,10},{10,2},{3,11},{11,3},{4,12},{12,4},... | collective-permute-start | bytes 147464 | tf_op jit(solution)/shard_map/ppermute | solution.py:323
  113.2 0.6 copy-start.21
  113.2 0.8 copy-start.4
